TPU v7x, 32 devices: a whole 2x2x4 slice. The times are simulated.
32 devices in a mesh: dp: 8 (over z, core), tp: 4 (over y, x).
Axes of the slice: x: 2, y: 2, z: 4, core: 2. Of those that a mesh axis runs over, the one named last changes fastest.
Arguments:
- hidden_states: bfloat16 [2048, 3584], P('dp'), may hold values from -21 to 21
- resp_lengths: int32 [4], replicated, may hold values from 1 to 1280, 2048 in all
- w_query: bfloat16 [3584, 512], P('dp', 'tp'), may hold values from -0.25 to 0.25
- w_keyval: bfloat16 [3584, 1024], P('dp', 'tp'), may hold values from -0.09375 to 0.09375
- w_out: bfloat16 [512, 3584], P('tp', 'dp'), may hold values from -0.25 to 0.25
Outputs:
- attended: bfloat16 [2048, 3584], P('dp', 'tp')
Inputs may be any that keep to these rules, and one draw needn't show every extreme that they name: `resp_lengths`: the 4 lengths sum to 2048; the longest is exactly 1280.
All inputs are finite; a program needn't handle non-finite values.
Results may differ from a plain program's by a relative error of at most 0.015.
The roundings to bfloat16 on the way count: a program that leaves them out, or rounds other values in their place, can miss the bound.
Values may be sent and summed in bfloat16 or wider, within the bound.
A program may use at most 64 MiB of HBM per device.

v0:
```python
import functools

import jax
import jax.numpy as jnp
from jax import lax
from jax.experimental import pallas as pl
from jax.experimental.pallas import tpu as pltpu
from jax.sharding import PartitionSpec as P

HD = 128


def segment_of(position, resp_ends):
    return jnp.sum(
        (position[:, None] >= resp_ends[None, :]).astype(jnp.int32), axis=1, dtype=jnp.int32
    )


def body(hidden_states, resp_lengths, w_query, w_keyval, w_out):
    token_rows = hidden_states.shape[0]
    head_scale = HD ** (-0.5)
    pieces = (
        lax.all_gather(w_query, "dp", axis=0, tiled=True),
        lax.all_gather(w_keyval, "dp", axis=0, tiled=True),
    )
    query_sum = jnp.dot(hidden_states, pieces[0], preferred_element_type=jnp.float32)
    keyval_sum = jnp.dot(hidden_states, pieces[1], preferred_element_type=jnp.float32)
    query = (query_sum * head_scale).astype(jnp.bfloat16)
    keyval = lax.all_gather(keyval_sum.astype(jnp.bfloat16), "tp", axis=1, tiled=True)
    kv_count = keyval.shape[1] // (2 * HD)
    per_group = lax.axis_size("tp") // kv_count
    kv_head = lax.axis_index("tp") // per_group
    key_head = lax.dynamic_slice_in_dim(keyval, kv_head * HD, HD, 1)
    value_head = lax.dynamic_slice_in_dim(keyval, (kv_count + kv_head) * HD, HD, 1)
    head_pair = jnp.concatenate([key_head, value_head], axis=1)
    resp_ends = jnp.cumsum(resp_lengths, dtype=jnp.int32)
    own_begin = lax.axis_index("dp") * token_rows
    query_pos = own_begin + jnp.arange(token_rows, dtype=jnp.int32)
    query_seg = segment_of(query_pos, resp_ends)
    pieces = lax.all_gather(head_pair, "dp", axis=0, tiled=True)
    largest = jnp.full((token_rows,), -1e30, jnp.float32)
    height = pieces.shape[0]
    key_pos = jnp.arange(height, dtype=jnp.int32)
    key_seg = segment_of(key_pos, resp_ends)
    scores = jnp.dot(query, pieces[:, :HD].T, preferred_element_type=jnp.float32)
    allowed = (
        (query_seg[:, None] == key_seg[None, :])
        & (key_pos[None, :] <= query_pos[:, None])
        & (key_pos[None, :] >= 0)
    )
    newest = jnp.maximum(largest, jnp.max(jnp.where(allowed, scores, jnp.float32(-1e30)), axis=1))
    expw = jnp.where(allowed, jnp.exp(scores - newest[:, None]), jnp.float32(0.0))
    denom = jnp.sum(expw, axis=1)
    numer = jnp.dot(expw.astype(jnp.bfloat16), pieces[:, HD:], preferred_element_type=jnp.float32)
    heads_out = (numer / denom[:, None]).astype(jnp.bfloat16)
    terms = jnp.dot(
        heads_out,
        lax.all_gather(w_out, "dp", axis=1, tiled=True),
        preferred_element_type=jnp.float32,
    )
    summed = lax.psum_scatter(terms.astype(jnp.bfloat16), "tp", scatter_dimension=1, tiled=True)
    return summed


MESH = pl.DeviceIdType.MESH
KVA, KVB, WQ, WO, KEY, VAL = range(6)


def fused_kernel(
    nz, nt, lens_ref, hid_hbm, wq_hbm, wkv_hbm, wo_hbm, out_ref,
    hid, wq, wkv, woc, wof, kvloc, kvb, kvacc, qacc, qbuf, scores, mref, lref, oacc, hloc, hcat,
    loc_sem, ss, rs, prs, kv_ss, kv_rs, wi_ss, wi_rs, wp_ss, wp_rs, h_ss, h_rs,
):
    dp = lax.axis_index("dp")
    t = lax.axis_index("tp")
    z, c = dp // 2, dp % 2
    rows = hid.shape[0]
    shard = wq_hbm.shape[0]
    half = shard // 2
    nout = wo_hbm.shape[0]

    loads = [
        pltpu.make_async_copy(wkv_hbm, wkv.at[pl.ds(dp * shard, shard)], loc_sem.at[0]),
        pltpu.make_async_copy(wq_hbm, wq.at[pl.ds(dp * shard, shard)], loc_sem.at[1]),
        pltpu.make_async_copy(hid_hbm, hid, loc_sem.at[2]),
        pltpu.make_async_copy(wo_hbm, woc.at[z], loc_sem.at[3]),
    ]
    for load in loads:
        load.start()

    barrier = pltpu.get_barrier_semaphore()
    partner = {"dp": dp + 1 - 2 * c, "tp": t}
    up, down = {"dp": dp + 2, "tp": t}, {"dp": dp - 2, "tp": t}
    has_up, has_down = z < nz - 1, z > 0
    pl.semaphore_signal(barrier, 1, device_id=partner, device_id_type=MESH)

    @pl.when(has_up)
    def _():
        pl.semaphore_signal(barrier, 1, device_id=up, device_id_type=MESH)

    @pl.when(has_down)
    def _():
        pl.semaphore_signal(barrier, 1, device_id=down, device_id_type=MESH)

    for k in range(1, nt):
        pl.semaphore_signal(
            barrier, 1, device_id={"dp": dp, "tp": (t + k) % nt}, device_id_type=MESH
        )
    pl.semaphore_wait(barrier, nt + has_up.astype(jnp.int32) + has_down.astype(jnp.int32))

    def slot(item, zz, cc):
        if item == KVA:
            return wkv.at[pl.ds((2 * zz + cc) * shard, half)]
        if item == KVB:
            return wkv.at[pl.ds((2 * zz + cc) * shard + half, half)]
        if item == WQ:
            return wq.at[pl.ds((2 * zz + cc) * shard, shard)]
        if item == WO:
            return woc.at[zz]
        return kvb.at[2 * zz + cc, 0 if item == KEY else 1]

    def chain(item, zz, way):
        ref = slot(item, zz, c)
        if way == 2:
            recv, to = prs.at[item, zz], partner
        else:
            recv, to = rs.at[item, zz], (up if way == 0 else down)
        return pltpu.make_async_remote_copy(
            ref, ref, ss.at[item, zz, way], recv, device_id=to, device_id_type=MESH
        )

    def from_chain(item, zz):
        ref = slot(item, zz, c)
        pltpu.make_async_remote_copy(
            ref, ref, ss.at[item, zz, 0], rs.at[item, zz], device_id=partner, device_id_type=MESH
        ).wait_recv()

    def from_partner(item, zz):
        ref = slot(item, zz, 1 - c)
        pltpu.make_async_remote_copy(
            ref, ref, ss.at[item, zz, 2], prs.at[item, zz], device_id=partner, device_id_type=MESH
        ).wait_recv()

    def own_moves(item, act):
        @pl.when(has_up)
        def _():
            act(chain(item, z, 0))

        if item not in (KEY, VAL):
            @pl.when(has_down)
            def _():
                act(chain(item, z, 1))

        if item in (KEY, VAL):
            @pl.when(c == 0)
            def _():
                act(chain(item, z, 2))
        elif item != WO:
            act(chain(item, z, 2))

    def passed_moves(item, k, below, act):
        zz = z - k if below else z + k
        if below:
            @pl.when(has_up)
            def _():
                act(chain(item, zz, 0))
        else:
            @pl.when(has_down)
            def _():
                act(chain(item, zz, 1))
        if item != WO:
            act(chain(item, zz, 2))

    def start(copy):
        copy.start()

    def wait_send(copy):
        copy.wait_send()

    def wo_block(g, cc):
        return wof.at[pl.ds(pl.multiple_of(cc * nout, 16), nout), pl.ds(pl.multiple_of(g * HD, HD), HD)]

    def in_plane(zz):
        return pltpu.make_async_remote_copy(
            woc.at[zz], wo_block(t, c), wi_ss.at[zz], wi_rs.at[t],
            device_id={"dp": dp, "tp": zz}, device_id_type=MESH,
        )

    def take_wo(zz):
        @pl.when(zz != t)
        def _():
            in_plane(zz).start()

        @pl.when(zz == t)
        def _():
            wo_block(t, c)[...] = woc[zz]
            own_wo(zz).start()

    def own_wo(zz):
        return pltpu.make_async_remote_copy(
            woc.at[zz], wo_block(t, c), wp_ss.at[t], wp_rs.at[t],
            device_id=partner, device_id_type=MESH,
        )

    def pass_on(item, k):
        @pl.when(z - k >= 0)
        def _():
            from_chain(item, z - k)
            passed_moves(item, k, True, start)
            if item == WO:
                take_wo(z - k)

        if item not in (KEY, VAL):
            @pl.when(z + k < nz)
            def _():
                from_chain(item, z + k)
                passed_moves(item, k, False, start)
                if item == WO:
                    take_wo(z + k)

    def each_side(k, fn):
        @pl.when(z - k >= 0)
        def _():
            fn(z - k)

        @pl.when(z + k < nz)
        def _():
            fn(z + k)

    def hidden_part(zz):
        return hid[:, pl.ds(pl.multiple_of(zz * 2 * shard, 128), 2 * shard)]

    def add_kv(zz):
        from_partner(KVA, zz)
        from_partner(KVB, zz)
        weights = wkv[pl.ds(pl.multiple_of(zz * 2 * shard, 16), 2 * shard), :]
        kvacc[...] += jnp.dot(hidden_part(zz), weights, preferred_element_type=jnp.float32)

    def add_q(zz):
        from_partner(WQ, zz)
        weights = wq[pl.ds(pl.multiple_of(zz * 2 * shard, 16), 2 * shard), :]
        qacc[...] += jnp.dot(hidden_part(zz), weights, preferred_element_type=jnp.float32)

    loads[0].wait()
    own_moves(KVA, start)
    own_moves(KVB, start)
    loads[2].wait()
    kvacc[...] = jnp.zeros_like(kvacc)
    qacc[...] = jnp.zeros_like(qacc)
    add_kv(z)
    for k in range(1, nz):
        pass_on(KVA, k)
        pass_on(KVB, k)
        if k == nz - 1:
            loads[1].wait()
            own_moves(WQ, start)
            loads[3].wait()
            own_moves(WO, start)
            take_wo(z)
        each_side(k, add_kv)

    role = t // (nt // 2)
    for h in range(2):
        kvloc[h] = kvacc[:, h * HD:(h + 1) * HD].astype(jnp.bfloat16)

    def kv_send(h):
        return pltpu.make_async_remote_copy(
            kvloc.at[h], kvb.at[dp, role], kv_ss.at[h], kv_rs.at[role],
            device_id={"dp": dp, "tp": 2 * (t % (nt // 2)) + h}, device_id_type=MESH,
        )

    for h in range(2):
        to = 2 * (t % (nt // 2)) + h

        @pl.when(to != t)
        def _():
            kv_send(h).start()

        @pl.when(to == t)
        def _():
            kvb[dp, role] = kvloc[h]

    add_q(z)
    for k in range(1, nz):
        pass_on(WQ, k)
        if k == 1:
            for r in range(2):
                @pl.when(t // 2 + r * (nt // 2) != t)
                def _():
                    pltpu.make_async_remote_copy(
                        kvloc.at[r], kvb.at[dp, r], kv_ss.at[r], kv_rs.at[r],
                        device_id=partner, device_id_type=MESH,
                    ).wait_recv()

            own_moves(KEY, start)
            own_moves(VAL, start)

            @pl.when(c == 0)
            def _():
                kvb[dp + 1] = jnp.zeros(kvb.shape[1:], kvb.dtype)

        pass_on(WO, k)
        each_side(k, add_q)
    qbuf[...] = (qacc[...] * (HD ** -0.5)).astype(jnp.bfloat16)

    qpos = dp * rows + lax.broadcasted_iota(jnp.int32, (rows, 1), 0)
    first = jnp.zeros((rows, 1), jnp.int32)
    end = jnp.int32(0)
    for r in range(lens_ref.shape[0]):
        end = end + lens_ref[r]
        first = jnp.where(qpos >= end, end, first)

    def pair(zz, which):
        return jnp.concatenate([kvb[2 * zz, which], kvb[2 * zz + 1, which]], axis=0)

    def score(zz):
        s = lax.dot_general(
            qbuf[...], pair(zz, 0), (((1,), (1,)), ((), ())), preferred_element_type=jnp.float32
        )
        kpos = zz * 2 * rows + lax.broadcasted_iota(jnp.int32, s.shape, 1)
        s = jnp.where((kpos >= first) & (kpos <= qpos), s, jnp.float32(-1e30))
        scores[zz] = s
        mref[...] = jnp.maximum(mref[...], jnp.max(s, axis=1, keepdims=True))

    mref[...] = jnp.full_like(mref, -1e30)
    for k in range(nz):
        if k == 0:
            @pl.when(c == 1)
            def _():
                from_partner(KEY, z)
            score(z)
        else:
            pass_on(KEY, k)
            pass_on(VAL, k)

            @pl.when(z - k >= 0)
            def _():
                from_partner(KEY, z - k)
                score(z - k)

    lref[...] = jnp.zeros_like(lref)
    oacc[...] = jnp.zeros_like(oacc)

    def weigh(zz, k):
        if k > 0:
            from_partner(VAL, zz)
        else:
            @pl.when(c == 1)
            def _():
                from_partner(VAL, zz)
        p = jnp.exp(scores[zz] - mref[...])
        lref[...] += jnp.sum(p, axis=1, keepdims=True)
        oacc[...] += jnp.dot(p.astype(jnp.bfloat16), pair(zz, 1), preferred_element_type=jnp.float32)

    for k in range(nz):
        @pl.when(z - k >= 0)
        def _():
            weigh(z - k, k)

    def head_cols(g):
        return hcat.at[:, pl.ds(pl.multiple_of(g * HD, HD), HD)]

    heads = (oacc[...] / lref[...]).astype(jnp.bfloat16)
    hloc[...] = heads
    head_cols(t)[...] = heads

    def head_copy(k):
        return pltpu.make_async_remote_copy(
            hloc, head_cols(t), h_ss.at[k], h_rs.at[t],
            device_id={"dp": dp, "tp": (t + k) % nt}, device_id_type=MESH,
        )

    for k in range(1, nt):
        head_copy(k).start()

    def wo_partner(g):
        return pltpu.make_async_remote_copy(
            wo_block(g, c), wo_block(g, c), wp_ss.at[g], wp_rs.at[g],
            device_id=partner, device_id_type=MESH,
        )

    for k in range(1, nt):
        g = (t + k) % nt
        pltpu.make_async_remote_copy(
            woc.at[0], wo_block(g, c), wi_ss.at[0], wi_rs.at[g],
            device_id=partner, device_id_type=MESH,
        ).wait_recv()
        wo_partner(g).start()
    for g in range(nt):
        pltpu.make_async_remote_copy(
            woc.at[0], wo_block(g, 1 - c), wp_ss.at[g], wp_rs.at[g],
            device_id=partner, device_id_type=MESH,
        ).wait_recv()
    for k in range(1, nt):
        g = (t + k) % nt
        pltpu.make_async_remote_copy(
            hloc, head_cols(g), h_ss.at[k], h_rs.at[g], device_id=partner, device_id_type=MESH
        ).wait_recv()
    out_ref[...] = lax.dot_general(
        hcat[...], wof[...], (((1,), (1,)), ((), ())), preferred_element_type=jnp.float32
    ).astype(out_ref.dtype)

    for item in (KVA, KVB, WQ, WO, KEY, VAL):
        own_moves(item, wait_send)
        for k in range(1, nz):
            @pl.when(z - k >= 0)
            def _():
                passed_moves(item, k, True, wait_send)

            if item not in (KEY, VAL):
                @pl.when(z + k < nz)
                def _():
                    passed_moves(item, k, False, wait_send)
    for h in range(2):
        @pl.when(2 * (t % (nt // 2)) + h != t)
        def _():
            kv_send(h).wait_send()
    for k in range(1, nt):
        head_copy(k).wait_send()
        wo_partner((t + k) % nt).wait_send()
        in_plane((t + k) % nt).wait_send()
    own_wo(t).wait_send()


def fused_body(nz, nt, hidden_states, resp_lengths, w_query, w_keyval, w_out):
    rows, depth = hidden_states.shape
    nout = w_out.shape[1]
    bf16, f32 = jnp.bfloat16, jnp.float32
    dma = pltpu.SemaphoreType.DMA
    hbm = pl.BlockSpec(memory_space=pltpu.HBM)
    return pl.pallas_call(
        functools.partial(fused_kernel, nz, nt),
        out_shape=jax.ShapeDtypeStruct((rows, 2 * nout), bf16),
        in_specs=[pl.BlockSpec(memory_space=pltpu.SMEM), hbm, hbm, hbm, hbm],
        out_specs=pl.BlockSpec(memory_space=pltpu.VMEM),
        scratch_shapes=[
            pltpu.VMEM((rows, depth), bf16),
            pltpu.VMEM((depth, w_query.shape[1]), bf16),
            pltpu.VMEM((depth, w_keyval.shape[1]), bf16),
            pltpu.VMEM((nz, nout, HD), bf16),
            pltpu.VMEM((2 * nout, nt * HD), bf16),
            pltpu.VMEM((2, rows, HD), bf16),
            pltpu.VMEM((2 * nz, 2, rows, HD), bf16),
            pltpu.VMEM((rows, 2 * HD), f32),
            pltpu.VMEM((rows, HD), f32),
            pltpu.VMEM((rows, HD), bf16),
            pltpu.VMEM((nz, rows, 2 * rows), f32),
            pltpu.VMEM((rows, 1), f32),
            pltpu.VMEM((rows, 1), f32),
            pltpu.VMEM((rows, HD), f32),
            pltpu.VMEM((rows, HD), bf16),
            pltpu.VMEM((rows, nt * HD), bf16),
            dma((4,)),
            dma((6, nz, 3)),
            dma((6, nz)),
            dma((6, nz)),
            dma((2,)),
            dma((2,)),
            dma((nz,)),
            dma((nt,)),
            dma((nt,)),
            dma((nt,)),
            dma((nt,)),
            dma((nt,)),
        ],
        compiler_params=pltpu.CompilerParams(
            collective_id=0, has_side_effects=True, vmem_limit_bytes=67_000_000
        ),
    )(resp_lengths, hidden_states, w_query, w_keyval, w_out.T)


def per_device(mesh, hidden_states, resp_lengths, w_query, w_keyval, w_out):
    nt = mesh.shape["tp"]
    nz = mesh.shape["dp"] // 2
    args = (hidden_states, resp_lengths, w_query, w_keyval, w_out)
    fits = (
        mesh.shape["dp"] == 2 * nz and nz == nt and nt % 2 == 0
        and w_query.shape[1] == HD and w_keyval.shape[1] == 2 * HD
        and w_out.shape[0] == HD and w_query.shape[0] % 64 == 0
    )
    return fused_body(nz, nt, *args) if fits else body(*args)


def solution(mesh):
    return jax.shard_map(
        functools.partial(per_device, mesh),
        mesh=mesh,
        in_specs=(P("dp", None), P(), P("dp", "tp"), P("dp", "tp"), P("tp", "dp")),
        out_specs=P("dp", "tp"),
        check_vma=False,
    )
```

profile of v0, /device:TPU:25, one launch (start us, length us, event | category | flops | bytes accessed | tf_op | source)
XLA Modules:
  0.0 53.1 jit_solution(2214421337764863038)
XLA Ops:
  0.0 51.2 %shard_map.55 = bf16[256,896]{1,0:T(8,128)(2,1)} custom-call(s32[4]{0:T(128)} %lens_ref.1, bf16[256,3584]{1,0:T(8,128)(2,1)} %hid_hbm.1, bf16[448,128]{1,0:T(8,128)(2,1)} %wq_hbm.1, bf16[448,256]{1,0:T(8,128)(2,1)} %wkv_hbm.1, bf16[448,128]{1,0:T(8,128)(2,1)} %bitcast.1), custom_call_target="tpu_custom_call" | custom-call | tf_op jit(solution)/shard_map/pallas_call | solution.py:431
  51.2 1.8 %copy.7 = bf16[256,896]{1,0:T(8,128)(2,1)} copy(bf16[256,896]{1,0:T(8,128)(2,1)} %shard_map.55) | data formatting | bytes 917504
where the time goes:
time: 53.2 us; the launch traced here: 53.1 us
  Pallas kernels  51.2 us (96%)
  local copies, waits for them, and re-layouts  1.82 us (3%)
    pallas_call x1, Pallas kernels, fused_body(): pl.pallas_call(functools.partial(fused_kernel, nz, nt), out_shape=jax.Sha...  51.2 us
    unnamed x1, local copies, waits for them, and re-layouts  1.82 us

commit v1 on v0

v1 whole, which is shorter than its diff:
```python
import functools

import jax
import jax.numpy as jnp
from jax import lax
from jax.experimental import pallas as pl
from jax.experimental.pallas import tpu as pltpu
from jax.sharding import PartitionSpec as P

HD = 128


def segment_of(position, resp_ends):
    return jnp.sum(
        (position[:, None] >= resp_ends[None, :]).astype(jnp.int32), axis=1, dtype=jnp.int32
    )


def body(hidden_states, resp_lengths, w_query, w_keyval, w_out):
    token_rows = hidden_states.shape[0]
    head_scale = HD ** (-0.5)
    pieces = (
        lax.all_gather(w_query, "dp", axis=0, tiled=True),
        lax.all_gather(w_keyval, "dp", axis=0, tiled=True),
    )
    query_sum = jnp.dot(hidden_states, pieces[0], preferred_element_type=jnp.float32)
    keyval_sum = jnp.dot(hidden_states, pieces[1], preferred_element_type=jnp.float32)
    query = (query_sum * head_scale).astype(jnp.bfloat16)
    keyval = lax.all_gather(keyval_sum.astype(jnp.bfloat16), "tp", axis=1, tiled=True)
    kv_count = keyval.shape[1] // (2 * HD)
    per_group = lax.axis_size("tp") // kv_count
    kv_head = lax.axis_index("tp") // per_group
    key_head = lax.dynamic_slice_in_dim(keyval, kv_head * HD, HD, 1)
    value_head = lax.dynamic_slice_in_dim(keyval, (kv_count + kv_head) * HD, HD, 1)
    head_pair = jnp.concatenate([key_head, value_head], axis=1)
    resp_ends = jnp.cumsum(resp_lengths, dtype=jnp.int32)
    own_begin = lax.axis_index("dp") * token_rows
    query_pos = own_begin + jnp.arange(token_rows, dtype=jnp.int32)
    query_seg = segment_of(query_pos, resp_ends)
    pieces = lax.all_gather(head_pair, "dp", axis=0, tiled=True)
    largest = jnp.full((token_rows,), -1e30, jnp.float32)
    height = pieces.shape[0]
    key_pos = jnp.arange(height, dtype=jnp.int32)
    key_seg = segment_of(key_pos, resp_ends)
    scores = jnp.dot(query, pieces[:, :HD].T, preferred_element_type=jnp.float32)
    allowed = (
        (query_seg[:, None] == key_seg[None, :])
        & (key_pos[None, :] <= query_pos[:, None])
        & (key_pos[None, :] >= 0)
    )
    newest = jnp.maximum(largest, jnp.max(jnp.where(allowed, scores, jnp.float32(-1e30)), axis=1))
    expw = jnp.where(allowed, jnp.exp(scores - newest[:, None]), jnp.float32(0.0))
    denom = jnp.sum(expw, axis=1)
    numer = jnp.dot(expw.astype(jnp.bfloat16), pieces[:, HD:], preferred_element_type=jnp.float32)
    heads_out = (numer / denom[:, None]).astype(jnp.bfloat16)
    terms = jnp.dot(
        heads_out,
        lax.all_gather(w_out, "dp", axis=1, tiled=True),
        preferred_element_type=jnp.float32,
    )
    summed = lax.psum_scatter(terms.astype(jnp.bfloat16), "tp", scatter_dimension=1, tiled=True)
    return summed


MESH = pl.DeviceIdType.MESH
KA, KB, WQ = range(3)
UP, DOWN, SIDE = range(3)
NEG = -1e30


def fused_kernel(
    nz, nt, lens_ref, hid_hbm, wq_hbm, wkv_hbm, wo_hbm, out_ref,
    hid, w, woc, wof, kvloc, kvb, acc, qb, part, lse, pin, lin, hloc, hcat,
    loc_sem, ss, rs, prs, kv_ss, kv_rs, kp_ss, kp_rs, wi_ss, wi_rs, wp_ss, wp_rs,
    pt_ss, pt_rs, h_ss, h_rs,
):
    dp = lax.axis_index("dp")
    t = lax.axis_index("tp")
    plane_of, c = dp // 2, dp % 2
    rows = hid.shape[0]
    shard = wq_hbm.shape[0]
    nout = wo_hbm.shape[0]
    own = pl.ds(pl.multiple_of(dp * shard, 64), shard)

    loads = [
        pltpu.make_async_copy(wkv_hbm.at[:, pl.ds(0, HD)], w.at[KA, own], loc_sem.at[KA]),
        pltpu.make_async_copy(wkv_hbm.at[:, pl.ds(HD, HD)], w.at[KB, own], loc_sem.at[KB]),
        pltpu.make_async_copy(wq_hbm, w.at[WQ, own], loc_sem.at[WQ]),
        pltpu.make_async_copy(hid_hbm, hid, loc_sem.at[3]),
        pltpu.make_async_copy(wo_hbm, woc, loc_sem.at[4]),
    ]
    for load in loads:
        load.start()

    barrier = pltpu.get_barrier_semaphore()
    partner = {"dp": dp + 1 - 2 * c, "tp": t}
    above, below = {"dp": dp + 2, "tp": t}, {"dp": dp - 2, "tp": t}
    has_up, has_down = plane_of < nz - 1, plane_of > 0
    pl.semaphore_signal(barrier, 1, device_id=partner, device_id_type=MESH)

    @pl.when(has_up)
    def _():
        pl.semaphore_signal(barrier, 1, device_id=above, device_id_type=MESH)

    @pl.when(has_down)
    def _():
        pl.semaphore_signal(barrier, 1, device_id=below, device_id_type=MESH)

    for k in range(1, nt):
        pl.semaphore_signal(
            barrier, 1, device_id={"dp": dp, "tp": (t + k) % nt}, device_id_type=MESH
        )
    pl.semaphore_wait(barrier, nt + has_up.astype(jnp.int32) + has_down.astype(jnp.int32))

    def chunk(item, zz, cc):
        return w.at[item, pl.ds(pl.multiple_of((2 * zz + cc) * shard, 64), shard)]

    def remote(src, dst, send, recv, to):
        return pltpu.make_async_remote_copy(
            src, dst, send, recv, device_id=to, device_id_type=MESH
        )

    def chain(item, zz, way):
        ref = chunk(item, zz, c)
        recv = prs.at[item, zz] if way == SIDE else rs.at[item, zz]
        return remote(ref, ref, ss.at[item, zz, way], recv, (above, below, partner)[way])

    def device(zz, tt):
        return {"dp": 2 * zz + c, "tp": tt}

    half_rows = pl.ds(pl.multiple_of(c * rows, 128), rows)
    other_rows = pl.ds(pl.multiple_of((1 - c) * rows, 128), rows)

    def kv_copy(z, b, zz):
        role = t // (nt // 2)
        return remote(
            kvloc.at[b], kvb.at[role, z, half_rows], kv_ss.at[b, zz], kv_rs.at[role, z],
            device(zz, 2 * (t % (nt // 2)) + b),
        )

    def kv_pass(z, role):
        ref = kvb.at[role, z, half_rows]
        return remote(ref, ref, kp_ss.at[role, z], kp_rs.at[role, z], partner)

    def kv_passed(z, role):
        ref = kvb.at[role, z, other_rows]
        return remote(ref, ref, kp_ss.at[role, z], kp_rs.at[role, z], partner)

    def wo_block(g, cc):
        return wof.at[
            pl.ds(pl.multiple_of(cc * nout, 64), nout), pl.ds(pl.multiple_of(g * HD, HD), HD)
        ]

    def wo_copy(z, zz):
        return remote(woc, wo_block(t, c), wi_ss.at[zz], wi_rs.at[t], device(zz, z))

    def wo_pass(g, cc):
        ref = wo_block(g, cc)
        return remote(ref, ref, wp_ss.at[g], wp_rs.at[g], partner)

    def head_cols(g):
        return hcat.at[:, pl.ds(pl.multiple_of(g * HD, HD), HD)]

    def head_copy(k):
        return remote(
            hloc, head_cols(t), h_ss.at[k], h_rs.at[t], {"dp": dp, "tp": (t + k) % nt}
        )

    ends = []
    end = jnp.int32(0)
    for r in range(lens_ref.shape[0]):
        end = end + lens_ref[r]
        ends.append(end)

    def plane(z):
        sent = []
        seen = set()
        top, bottom = z == nz - 1, z == 0
        kv_to = [zz for zz in (nz - 2, nz - 3, 0) if zz >= z] if not top else [z]
        span = 2 * shard

        def go(copy):
            copy.start()
            sent.append(copy)

        def own_send(item, way):
            go(chain(item, z, way))

        def event(item, zz, *ways):
            ref = chunk(item, zz, c)
            remote(ref, ref, ss.at[item, zz, UP], rs.at[item, zz], partner).wait_recv()
            for way in ways + (SIDE,):
                go(chain(item, zz, way))

        def dot(item, zz):
            ref = chunk(item, zz, 1 - c)
            remote(ref, ref, ss.at[item, zz, SIDE], prs.at[item, zz], partner).wait_recv()
            part_sum = jnp.dot(
                hid[:, zz * span:(zz + 1) * span], w[item, zz * span:(zz + 1) * span, :],
                preferred_element_type=jnp.float32,
            )
            if item in seen:
                acc[item] += part_sum
            else:
                seen.add(item)
                acc[item] = part_sum

        def finish_kv(b):
            kvloc[b] = acc[b].astype(jnp.bfloat16)
            role = t // (nt // 2)
            for zz in kv_to:
                if zz != z:
                    go(kv_copy(z, b, zz))
            mine = 2 * (t % (nt // 2)) + b == t

            @pl.when(jnp.logical_not(mine))
            def _():
                kv_copy(z, b, z).start()

            @pl.when(mine)
            def _():
                kvb[role, z, half_rows, :] = kvloc[b]

        def end_kv():
            for b in range(2):
                @pl.when(2 * (t % (nt // 2)) + b != t)
                def _():
                    kv_copy(z, b, z).wait_send()

        def take_kv(zs):
            for role in range(2):
                arrived = remote(
                    kvloc.at[0], kvb.at[role, zs, half_rows], kv_ss.at[0, zs],
                    kv_rs.at[role, zs], partner,
                )
                if zs == z:
                    @pl.when(t // 2 + role * (nt // 2) != t)
                    def _():
                        arrived.wait_recv()
                else:
                    arrived.wait_recv()
                go(kv_pass(zs, role))

        def need_kv(zs):
            for role in range(2):
                kv_passed(zs, role).wait_recv()

        def finish_q():
            qb[0] = (acc[WQ] * (HD ** -0.5)).astype(jnp.bfloat16)

        def attend(state, qi, zs):
            qpos = (dp + 2 * qi) * rows + lax.broadcasted_iota(jnp.int32, (rows, 1), 0)
            first = jnp.zeros((rows, 1), jnp.int32)
            for e in ends:
                first = jnp.where(qpos >= e, e, first)
            s = lax.dot_general(
                qb[qi], kvb[0, zs], (((1,), (1,)), ((), ())), preferred_element_type=jnp.float32
            )
            kpos = zs * 2 * rows + lax.broadcasted_iota(jnp.int32, s.shape, 1)
            s = jnp.where((kpos >= first) & (kpos <= qpos), s, jnp.float32(NEG))
            peak = jnp.max(s, axis=1, keepdims=True)
            if state is not None:
                peak = jnp.maximum(state[0], peak)
            p = jnp.exp(s - peak)
            total = jnp.sum(p, axis=1, keepdims=True)
            value = jnp.dot(
                p.astype(jnp.bfloat16), kvb[1, zs], preferred_element_type=jnp.float32
            )
            if state is not None:
                fade = jnp.exp(state[0] - peak)
                total = total + state[1] * fade
                value = value + state[2] * fade
            return peak, total, value

        def wo_near():
            loads[4].wait()

            @pl.when(t != z)
            def _():
                wo_copy(z, z).start()

            @pl.when(t == z)
            def _():
                wo_block(t, c)[...] = woc[...]

        def wo_far(zz):
            go(wo_copy(z, zz))

        def query_copy():
            return remote(qb.at[0], qb.at[1], pt_ss.at[0], pt_rs.at[0], below)

        def part_copies(to):
            return (
                remote(part, pin, pt_ss.at[1], pt_rs.at[1], to),
                remote(lse, lin, pt_ss.at[2], pt_rs.at[2], to),
            )

        for item in (WQ, KA, KB):
            loads[item].wait()
            if not top and (bottom or item != KB):
                own_send(item, UP)
            if top or (not bottom and item != WQ):
                own_send(item, DOWN)
            own_send(item, SIDE)
        wo_near()
        loads[3].wait()

        waiting = [(WQ, z), (KA, z), (KB, z)]

        def step(item, zz, *ways, keep=2):
            event(item, zz, *ways)
            waiting.append((item, zz))
            settle(keep)

        def settle(keep):
            while len(waiting) > keep:
                dot(*waiting.pop(0))

        if bottom:
            for zz in range(1, nz):
                step(KA, zz)
                step(KB, zz)
                if zz == 1:
                    wo_far(1)
            settle(0)
            finish_kv(KA)
            finish_kv(KB)
            for zz in range(nz - 1, 1, -1):
                wo_far(zz)
            for zz in range(1, nz):
                step(WQ, zz, keep=1)
            take_kv(z)
            settle(0)
            finish_q()
            need_kv(z)
            state = attend(None, 0, z)
        elif top:
            step(WQ, 2)
            wo_far(2)
            step(KA, 2)
            step(WQ, 1)
            step(KB, 2)
            step(WQ, 0)
            settle(0)
            finish_q()
            go(query_copy())
            wo_far(1)
            step(KA, 1, keep=1)
            step(KB, 1, keep=1)
            wo_far(0)
            step(KA, 0, keep=1)
            step(KB, 0, keep=1)
            finish_kv(KA)
            settle(0)
            finish_kv(KB)
            take_kv(z)
            need_kv(z)
            peak, total, value = attend(None, 0, z)
            for copy in part_copies(below):
                copy.wait_recv()
            side = jnp.transpose(jnp.broadcast_to(lin[0:1, :], (HD, rows)))[:, 0:1]
            best = jnp.maximum(peak, side)
            near, far = jnp.exp(peak - best), jnp.exp(side - best)
            state = (
                best, total * near + far, value * near + pin[...].astype(jnp.float32) * far
            )
        elif z == 1:
            step(KA, 2, DOWN)
            step(WQ, 0, UP)
            own_send(KB, UP)
            step(KB, 2, DOWN)
            step(KA, 0, UP)
            step(KA, 3, DOWN)
            step(KB, 0, UP)
            step(KB, 3, DOWN)
            own_send(WQ, DOWN)
            settle(0)
            finish_kv(KA)
            finish_kv(KB)
            step(WQ, 2, DOWN)
            step(WQ, 3, DOWN)
            wo_far(0)
            take_kv(z)
            settle(0)
            finish_q()
            need_kv(z)
            state = attend(None, 0, z)
            take_kv(0)
            wo_far(2)
            wo_far(3)
            need_kv(0)
            state = attend(state, 0, 0)
        else:
            step(WQ, 1, UP)
            own_send(KB, UP)
            step(KA, 3, DOWN)
            step(KB, 3, DOWN)
            own_send(WQ, DOWN)
            step(KA, 1)
            step(WQ, 3, DOWN)
            wo_far(1)
            step(WQ, 0, UP)
            go(chain(KA, 1, UP))
            step(KB, 1, UP)
            step(KA, 0, UP)
            wo_far(0)
            step(KB, 0, UP)
            wo_far(3)
            settle(0)
            finish_kv(KA)
            finish_kv(KB)
            finish_q()
            take_kv(1)
            need_kv(1)
            state = attend(None, 0, 1)
            query_copy().wait_recv()
            other = attend(None, 1, 1)
            take_kv(z)
            need_kv(z)
            other = attend(other, 1, z)
            state = attend(state, 0, z)
            take_kv(0)
            need_kv(0)
            peak, total, value = attend(other, 1, 0)
            part[...] = (value / total).astype(jnp.bfloat16)
            lse[...] = jnp.transpose(
                jnp.broadcast_to(peak + jnp.log(total), (rows, HD))
            )[:lse.shape[0], :]
            for copy in part_copies(above):
                go(copy)
            state = attend(state, 0, 0)

        hloc[...] = (state[2] / state[1]).astype(jnp.bfloat16)
        for k in range(1, nt):
            head_copy(k).start()
        head_cols(t)[...] = hloc[...]

        for g in range(nt):
            arrived = remote(woc, wo_block(g, c), wi_ss.at[0], wi_rs.at[g], partner)
            if g == z:
                @pl.when(t != z)
                def _():
                    arrived.wait_recv()
            else:
                arrived.wait_recv()
            go(wo_pass(g, c))
        end_kv()

        @pl.when(t != z)
        def _():
            wo_copy(z, z).wait_send()

        for g in range(nt):
            wo_pass(g, 1 - c).wait_recv()
        for copy in sent:
            copy.wait_send()

    for z in range(nz):
        @pl.when(plane_of == z)
        def _():
            plane(z)

    for k in range(1, nt):
        head_copy(k).wait_send()
        g = (t + k) % nt
        remote(hloc, head_cols(g), h_ss.at[k], h_rs.at[g], partner).wait_recv()
    out_ref[...] = lax.dot_general(
        hcat[...], wof[...], (((1,), (1,)), ((), ())), preferred_element_type=jnp.float32
    ).astype(out_ref.dtype)


def fused_body(nz, nt, hidden_states, resp_lengths, w_query, w_keyval, w_out):
    rows, depth = hidden_states.shape
    nout = w_out.shape[1]
    bf16, f32 = jnp.bfloat16, jnp.float32
    dma = pltpu.SemaphoreType.DMA
    hbm = pl.BlockSpec(memory_space=pltpu.HBM)
    return pl.pallas_call(
        functools.partial(fused_kernel, nz, nt),
        out_shape=jax.ShapeDtypeStruct((rows, 2 * nout), bf16),
        in_specs=[pl.BlockSpec(memory_space=pltpu.SMEM), hbm, hbm, hbm, hbm],
        out_specs=pl.BlockSpec(memory_space=pltpu.VMEM),
        scratch_shapes=[
            pltpu.VMEM((rows, depth), bf16),
            pltpu.VMEM((3, depth, HD), bf16),
            pltpu.VMEM((nout, HD), bf16),
            pltpu.VMEM((2 * nout, nt * HD), bf16),
            pltpu.VMEM((2, rows, HD), bf16),
            pltpu.VMEM((2, nz, 2 * rows, HD), bf16),
            pltpu.VMEM((3, rows, HD), f32),
            pltpu.VMEM((2, rows, HD), bf16),
            pltpu.VMEM((rows, HD), bf16),
            pltpu.VMEM((8, rows), f32),
            pltpu.VMEM((rows, HD), bf16),
            pltpu.VMEM((8, rows), f32),
            pltpu.VMEM((rows, HD), bf16),
            pltpu.VMEM((rows, nt * HD), bf16),
            dma((5,)),
            dma((3, nz, 3)),
            dma((3, nz)),
            dma((3, nz)),
            dma((2, nz)),
            dma((2, nz)),
            dma((2, nz)),
            dma((2, nz)),
            dma((nz,)),
            dma((nt,)),
            dma((nt,)),
            dma((nt,)),
            dma((3,)),
            dma((3,)),
            dma((nt,)),
            dma((nt,)),
        ],
        compiler_params=pltpu.CompilerParams(
            collective_id=0, has_side_effects=True, vmem_limit_bytes=67_000_000
        ),
    )(resp_lengths, hidden_states, w_query, w_keyval, w_out.T)


def per_device(mesh, hidden_states, resp_lengths, w_query, w_keyval, w_out):
    nt = mesh.shape["tp"]
    nz = mesh.shape["dp"] // 2
    args = (hidden_states, resp_lengths, w_query, w_keyval, w_out)
    fits = (
        mesh.shape["dp"] == 2 * nz and nz == nt and nt == 4
        and w_query.shape[1] == HD and w_keyval.shape[1] == 2 * HD
        and w_out.shape[0] == HD and w_query.shape[0] % 64 == 0
    )
    return fused_body(nz, nt, *args) if fits else body(*args)


def solution(mesh):
    return jax.shard_map(
        functools.partial(per_device, mesh),
        mesh=mesh,
        in_specs=(P("dp", None), P(), P("dp", "tp"), P("dp", "tp"), P("tp", "dp")),
        out_specs=P("dp", "tp"),
        check_vma=False,
    )
```

time: 53.2 us -> 51.2 us (0.962)
  the two profiles are of different devices: /device:TPU:25 before, /device:TPU:27 now
where the time goes in v1:
time: 51.2 us; the launch traced here: 51 us
  Pallas kernels  49.2 us (96%)
  local copies, waits for them, and re-layouts  1.82 us (4%)
    pallas_call x1, Pallas kernels, fused_body(): pl.pallas_call(functools.partial(fused_kernel, nz, nt), out_shape=jax.Sha...  49.2 us
    unnamed x1, local copies, waits for them, and re-layouts  1.82 us

profile of v1, /device:TPU:27, one launch (start us, length us, event | category | flops | bytes accessed | tf_op | source)
XLA Modules:
  0.0 51.0 jit_solution(12202282146314130833)
XLA Ops:
  0.0 49.2 %shard_map.55 = bf16[256,896]{1,0:T(8,128)(2,1)} custom-call(s32[4]{0:T(128)} %lens_ref.1, bf16[256,3584]{1,0:T(8,128)(2,1)} %hid_hbm.1, bf16[448,128]{1,0:T(8,128)(2,1)} %wq_hbm.1, bf16[448,256]{1,0:T(8,128)(2,1)} %wkv_hbm.1, bf16[448,128]{1,0:T(8,128)(2,1)} %bitcast.1), custom_call_target="tpu_custom_call" | custom-call | tf_op jit(solution)/shard_map/pallas_call | solution.py:478
  49.2 1.8 %copy.7 = bf16[256,896]{1,0:T(8,128)(2,1)} copy(bf16[256,896]{1,0:T(8,128)(2,1)} %shard_map.55) | data formatting | bytes 917504

commit v2 on v1

--- a/solution.py
+++ b/solution.py
@@ -69,10 +69,10 @@
 
 
 def fused_kernel(
-    nz, nt, lens_ref, hid_hbm, wq_hbm, wkv_hbm, wo_hbm, out_ref,
-    hid, w, woc, wof, kvloc, kvb, acc, qb, part, lse, pin, lin, hloc, hcat,
-    loc_sem, ss, rs, prs, kv_ss, kv_rs, kp_ss, kp_rs, wi_ss, wi_rs, wp_ss, wp_rs,
-    pt_ss, pt_rs, h_ss, h_rs,
+    nz, nt, lens_hbm, hid_hbm, wq_hbm, wkv_hbm, wo_hbm, out_ref,
+    hid, w, woc, wox, wof, kvloc, kvb, acc, qb, part, lse, pin, lin, hloc, hcat,
+    loc_sem, ss, rs, prs, kv_ss, kv_rs, kp_ss, kp_rs, wc_ss, wx_ss, wx_rs, wi_ss, wi_rs, wp_ss, wp_rs,
+    pt_ss, pt_rs, h_ss, h_rs, lens_ref,
 ):
     dp = lax.axis_index("dp")
     t = lax.axis_index("tp")
@@ -88,6 +88,7 @@
         pltpu.make_async_copy(wq_hbm, w.at[WQ, own], loc_sem.at[WQ]),
         pltpu.make_async_copy(hid_hbm, hid, loc_sem.at[3]),
         pltpu.make_async_copy(wo_hbm, woc, loc_sem.at[4]),
+        pltpu.make_async_copy(lens_hbm, lens_ref, loc_sem.at[5]),
     ]
     for load in loads:
         load.start()
@@ -151,8 +152,27 @@
             pl.ds(pl.multiple_of(cc * nout, 64), nout), pl.ds(pl.multiple_of(g * HD, HD), HD)
         ]
 
-    def wo_copy(z, zz):
-        return remote(woc, wo_block(t, c), wi_ss.at[zz], wi_rs.at[t], device(zz, z))
+    def wo_half(g, h):
+        start = pl.multiple_of(c * nout + h * (nout // 2), 16)
+        return wof.at[pl.ds(start, nout // 2), pl.ds(pl.multiple_of(g * HD, HD), HD)]
+
+    def wo_ref(g, way):
+        return wo_half(g, 0) if g == (nt - 1 if way == UP else 0) else wo_block(g, c)
+
+    def wo_chain(g, way):
+        ref = wo_ref(g, way)
+        return remote(ref, ref, wc_ss.at[g, way], wi_rs.at[g], (above, below)[way])
+
+    def wo_loose(src, zz, way):
+        return remote(src, wox.at[zz], wx_ss.at[zz, way], wx_rs.at[zz], (above, below)[way])
+
+    def wo_cross(zz):
+        return remote(woc, wo_block(t, c), wi_ss.at[zz], wi_rs.at[t], {"dp": dp, "tp": zz})
+
+    def wo_loose_cross(zz):
+        return remote(
+            wox.at[zz], wo_half(t, 1), wi_ss.at[zz], wx_rs.at[nz], {"dp": dp, "tp": zz}
+        )
 
     def wo_pass(g, cc):
         ref = wo_block(g, cc)
@@ -166,6 +186,7 @@
             hloc, head_cols(t), h_ss.at[k], h_rs.at[t], {"dp": dp, "tp": (t + k) % nt}
         )
 
+    loads[5].wait()
     ends = []
     end = jnp.int32(0)
     for r in range(lens_ref.shape[0]):
@@ -272,19 +293,54 @@
                 value = value + state[2] * fade
             return peak, total, value
 
-        def wo_near():
-            loads[4].wait()
-
-            @pl.when(t != z)
+        last = nt - 1
+
+        def go_if(cond, copy):
+            @pl.when(cond)
             def _():
-                wo_copy(z, z).start()
-
+                copy.start()
+            sent.append((cond, copy))
+
+        def wo_arrived(g, ref):
+            remote(ref, ref, wc_ss.at[g, UP], wi_rs.at[g], partner).wait_recv()
+
+        def collect():
             @pl.when(t == z)
             def _():
-                wo_block(t, c)[...] = woc[...]
-
-        def wo_far(zz):
-            go(wo_copy(z, zz))
+                for g in range(nt):
+                    if g != z:
+                        wo_arrived(g, wo_block(g, c))
+
+        def hub(way, *picks):
+            for k in picks:
+                go_if(t == z, wo_chain(k if way == UP else (k + 1) % nt, way))
+
+        def loose(way):
+            go_if(t == (last if way == UP else 0), wo_loose(woc.at[pl.ds(nout // 2, nout // 2)], z, way))
+
+        def relay(way, *picks):
+            if z == (0 if way == UP else nz - 1):
+                return
+            mine = t < z if way == UP else t > z
+            for k in picks:
+                g = k if way == UP else (k + 1) % nt
+
+                @pl.when(mine)
+                def _():
+                    wo_arrived(g, wo_ref(g, way))
+                if z != (nz - 1 if way == UP else 0):
+                    go_if(mine, wo_chain(g, way))
+
+        def relay_loose(way, zs):
+            mine = t == (last if way == UP else 0)
+
+            @pl.when(mine)
+            def _():
+                ref = wox.at[zs]
+                remote(ref, ref, wx_ss.at[zs, way], wx_rs.at[zs], partner).wait_recv()
+            if z != (nz - 1 if way == UP else 0):
+                go_if(mine, wo_loose(wox.at[zs], zs, way))
+            go_if(mine, wo_loose_cross(zs))
 
         def query_copy():
             return remote(qb.at[0], qb.at[1], pt_ss.at[0], pt_rs.at[0], below)
@@ -295,14 +351,21 @@
                 remote(lse, lin, pt_ss.at[2], pt_rs.at[2], to),
             )
 
-        for item in (WQ, KA, KB):
+        order = (KA, KB, WQ) if top else (WQ, KA, KB)
+        for item in order:
             loads[item].wait()
             if not top and (bottom or item != KB):
                 own_send(item, UP)
             if top or (not bottom and item != WQ):
                 own_send(item, DOWN)
             own_send(item, SIDE)
-        wo_near()
+        loads[4].wait()
+        go_if(t != z, wo_cross(z))
+
+        @pl.when(t == z)
+        def _():
+            wo_block(t, c)[...] = woc[...]
+
         loads[3].wait()
 
         waiting = [(WQ, z), (KA, z), (KB, z)]
@@ -317,16 +380,17 @@
                 dot(*waiting.pop(0))
 
         if bottom:
-            for zz in range(1, nz):
+            step(KA, 1)
+            collect()
+            loose(UP)
+            hub(UP, 0, 1, 2, 3)
+            step(KB, 1)
+            for zz in range(2, nz):
                 step(KA, zz)
                 step(KB, zz)
-                if zz == 1:
-                    wo_far(1)
             settle(0)
             finish_kv(KA)
             finish_kv(KB)
-            for zz in range(nz - 1, 1, -1):
-                wo_far(zz)
             for zz in range(1, nz):
                 step(WQ, zz, keep=1)
             take_kv(z)
@@ -336,18 +400,18 @@
             state = attend(None, 0, z)
         elif top:
             step(WQ, 2)
-            wo_far(2)
             step(KA, 2)
+            collect()
+            loose(DOWN)
+            hub(DOWN, 0, 1, 2, 3)
             step(WQ, 1)
             step(KB, 2)
             step(WQ, 0)
             settle(0)
             finish_q()
             go(query_copy())
-            wo_far(1)
             step(KA, 1, keep=1)
             step(KB, 1, keep=1)
-            wo_far(0)
             step(KA, 0, keep=1)
             step(KB, 0, keep=1)
             finish_kv(KA)
@@ -365,29 +429,39 @@
                 best, total * near + far, value * near + pin[...].astype(jnp.float32) * far
             )
         elif z == 1:
-            step(KA, 2, DOWN)
             step(WQ, 0, UP)
             own_send(KB, UP)
+            step(KA, 2, DOWN)
+            step(KA, 0, UP)
             step(KB, 2, DOWN)
-            step(KA, 0, UP)
             step(KA, 3, DOWN)
             step(KB, 0, UP)
             step(KB, 3, DOWN)
             own_send(WQ, DOWN)
+            collect()
             settle(0)
             finish_kv(KA)
             finish_kv(KB)
+            loose(UP)
+            hub(UP, 0)
+            relay(UP, 0)
+            relay_loose(UP, 0)
             step(WQ, 2, DOWN)
             step(WQ, 3, DOWN)
-            wo_far(0)
+            loose(DOWN)
+            hub(DOWN, 0, 1, 2, 3)
             take_kv(z)
             settle(0)
             finish_q()
             need_kv(z)
             state = attend(None, 0, z)
+            relay(DOWN, 0, 1)
+            relay_loose(DOWN, 2)
+            relay_loose(DOWN, 3)
             take_kv(0)
-            wo_far(2)
-            wo_far(3)
+            hub(UP, 1, 2, 3)
+            relay(UP, 1, 2, 3)
+            relay(DOWN, 2, 3)
             need_kv(0)
             state = attend(state, 0, 0)
         else:
@@ -398,18 +472,24 @@
             own_send(WQ, DOWN)
             step(KA, 1)
             step(WQ, 3, DOWN)
-            wo_far(1)
             step(WQ, 0, UP)
             go(chain(KA, 1, UP))
+            collect()
+            loose(DOWN)
+            hub(DOWN, 0, 1, 2, 3)
             step(KB, 1, UP)
+            relay(DOWN, 0)
+            relay_loose(DOWN, 3)
             step(KA, 0, UP)
-            wo_far(0)
+            relay(DOWN, 1)
             step(KB, 0, UP)
-            wo_far(3)
+            loose(UP)
+            hub(UP, 0)
             settle(0)
             finish_kv(KA)
             finish_kv(KB)
             finish_q()
+            relay(DOWN, 2, 3)
             take_kv(1)
             need_kv(1)
             state = attend(None, 0, 1)
@@ -419,6 +499,8 @@
             need_kv(z)
             other = attend(other, 1, z)
             state = attend(state, 0, z)
+            relay(UP, 0)
+            relay_loose(UP, 1)
             take_kv(0)
             need_kv(0)
             peak, total, value = attend(other, 1, 0)
@@ -428,6 +510,8 @@
             )[:lse.shape[0], :]
             for copy in part_copies(above):
                 go(copy)
+            hub(UP, 1, 2, 3)
+            relay_loose(UP, 0)
             state = attend(state, 0, 0)
 
         hloc[...] = (state[2] / state[1]).astype(jnp.bfloat16)
@@ -435,38 +519,49 @@
             head_copy(k).start()
         head_cols(t)[...] = hloc[...]
 
-        for g in range(nt):
-            arrived = remote(woc, wo_block(g, c), wi_ss.at[0], wi_rs.at[g], partner)
-            if g == z:
-                @pl.when(t != z)
-                def _():
-                    arrived.wait_recv()
-            else:
-                arrived.wait_recv()
-            go(wo_pass(g, c))
-        end_kv()
+        if bottom:
+            for zz in range(1, nz):
+                relay_loose(DOWN, zz)
+            relay(DOWN, 0, 1, 2, 3)
+        elif top:
+            for zz in range(nz - 2, -1, -1):
+                relay_loose(UP, zz)
+            relay(UP, 0, 1, 2, 3)
+        elif z == 2:
+            relay(UP, 1, 2, 3)
 
         @pl.when(t != z)
         def _():
-            wo_copy(z, z).wait_send()
-
+            ref = wox.at[0]
+            remote(ref, ref, wi_ss.at[z], wx_rs.at[nz], partner).wait_recv()
         for g in range(nt):
-            wo_pass(g, 1 - c).wait_recv()
+            wo_pass(g, c).start()
+        end_kv()
         for copy in sent:
-            copy.wait_send()
+            if isinstance(copy, tuple):
+                @pl.when(copy[0])
+                def _():
+                    copy[1].wait_send()
+            else:
+                copy.wait_send()
 
     for z in range(nz):
         @pl.when(plane_of == z)
         def _():
             plane(z)
 
+    for g in range(nt):
+        wo_pass(g, 1 - c).wait_recv()
     for k in range(1, nt):
-        head_copy(k).wait_send()
         g = (t + k) % nt
         remote(hloc, head_cols(g), h_ss.at[k], h_rs.at[g], partner).wait_recv()
     out_ref[...] = lax.dot_general(
         hcat[...], wof[...], (((1,), (1,)), ((), ())), preferred_element_type=jnp.float32
     ).astype(out_ref.dtype)
+    for k in range(1, nt):
+        head_copy(k).wait_send()
+    for g in range(nt):
+        wo_pass(g, c).wait_send()
 
 
 def fused_body(nz, nt, hidden_states, resp_lengths, w_query, w_keyval, w_out):
@@ -478,12 +573,13 @@
     return pl.pallas_call(
         functools.partial(fused_kernel, nz, nt),
         out_shape=jax.ShapeDtypeStruct((rows, 2 * nout), bf16),
-        in_specs=[pl.BlockSpec(memory_space=pltpu.SMEM), hbm, hbm, hbm, hbm],
+        in_specs=[hbm] * 5,
         out_specs=pl.BlockSpec(memory_space=pltpu.VMEM),
         scratch_shapes=[
             pltpu.VMEM((rows, depth), bf16),
             pltpu.VMEM((3, depth, HD), bf16),
             pltpu.VMEM((nout, HD), bf16),
+            pltpu.VMEM((nz, nout // 2, HD), bf16),
             pltpu.VMEM((2 * nout, nt * HD), bf16),
             pltpu.VMEM((2, rows, HD), bf16),
             pltpu.VMEM((2, nz, 2 * rows, HD), bf16),
@@ -495,7 +591,7 @@
             pltpu.VMEM((8, rows), f32),
             pltpu.VMEM((rows, HD), bf16),
             pltpu.VMEM((rows, nt * HD), bf16),
-            dma((5,)),
+            dma((6,)),
             dma((3, nz, 3)),
             dma((3, nz)),
             dma((3, nz)),
@@ -503,6 +599,9 @@
             dma((2, nz)),
             dma((2, nz)),
             dma((2, nz)),
+            dma((nt, 2)),
+            dma((nz, 2)),
+            dma((nz + 1,)),
             dma((nz,)),
             dma((nt,)),
             dma((nt,)),
@@ -511,11 +610,15 @@
             dma((3,)),
             dma((nt,)),
             dma((nt,)),
+            pltpu.SMEM(resp_lengths.shape, jnp.int32),
         ],
         compiler_params=pltpu.CompilerParams(
-            collective_id=0, has_side_effects=True, vmem_limit_bytes=67_000_000
+            collective_id=0, has_side_effects=True, vmem_limit_bytes=40_000_000
         ),
-    )(resp_lengths, hidden_states, w_query, w_keyval, w_out.T)
+    )(*[
+        pltpu.with_memory_space_constraint(x, pltpu.HBM)
+        for x in (resp_lengths, hidden_states, w_query, w_keyval, w_out.T)
+    ])
 
 
 def per_device(mesh, hidden_states, resp_lengths, w_query, w_keyval, w_out):

time: 51.2 us -> 45.7 us (0.89)
  the two profiles are of different devices: /device:TPU:27 before, /device:TPU:25 now
where the time goes in v2:
time: 45.7 us; the launch traced here: 45.1 us
  Pallas kernels  44.4 us (97%)
  local copies, waits for them, and re-layouts  0.77 us (2%)
    pallas_call x1, Pallas kernels, fused_body(): pl.pallas_call(functools.partial(fused_kernel, nz, nt), out_shape=jax.Sha...  44.4 us

profile of v2, /device:TPU:25, one launch (start us, length us, event | category | flops | bytes accessed | tf_op | source)
XLA Modules:
  0.0 45.1 jit_solution(12617788508410948483)
XLA Ops:
  0.0 44.4 %shard_map.55 = bf16[256,896]{1,0:T(8,128)(2,1)S(1)} custom-call(s32[4]{0:T(128)} %lens_hbm.1, bf16[256,3584]{1,0:T(8,128)(2,1)} %hid_hbm.1, bf16[448,128]{1,0:T(8,128)(2,1)} %wq_hbm.1, bf16[448,256]{1,0:T(8,128)(2,1)} %wkv_hbm.1, bf16[448,128]{1,0:T(8,128)(2,1)} %bitcast.1), custom_call_target="tpu_custom_call" | custom-call | tf_op jit(solution)/shard_map/pallas_call | solution.py:573
  44.4 0.8 %copy.7 = bf16[256,896]{1,0:T(8,128)(2,1)} copy(bf16[256,896]{1,0:T(8,128)(2,1)S(1)} %shard_map.55) | data formatting | bytes 917504

commit v3 on v2

--- a/solution.py
+++ b/solution.py
@@ -66,6 +66,7 @@
 KA, KB, WQ = range(3)
 UP, DOWN, SIDE = range(3)
 NEG = -1e30
+LOOSE = 6
 
 
 def fused_kernel(
@@ -152,9 +153,12 @@
             pl.ds(pl.multiple_of(cc * nout, 64), nout), pl.ds(pl.multiple_of(g * HD, HD), HD)
         ]
 
+    split = nout - wox.shape[1]
+
     def wo_half(g, h):
-        start = pl.multiple_of(c * nout + h * (nout // 2), 16)
-        return wof.at[pl.ds(start, nout // 2), pl.ds(pl.multiple_of(g * HD, HD), HD)]
+        start = pl.multiple_of(c * nout + h * split, 16)
+        size = nout - split if h else split
+        return wof.at[pl.ds(start, size), pl.ds(pl.multiple_of(g * HD, HD), HD)]
 
     def wo_ref(g, way):
         return wo_half(g, 0) if g == (nt - 1 if way == UP else 0) else wo_block(g, c)
@@ -316,7 +320,7 @@
                 go_if(t == z, wo_chain(k if way == UP else (k + 1) % nt, way))
 
         def loose(way):
-            go_if(t == (last if way == UP else 0), wo_loose(woc.at[pl.ds(nout // 2, nout // 2)], z, way))
+            go_if(t == (last if way == UP else 0), wo_loose(woc.at[pl.ds(split, nout - split)], z, way))
 
         def relay(way, *picks):
             if z == (0 if way == UP else nz - 1):
@@ -420,6 +424,8 @@
             take_kv(z)
             need_kv(z)
             peak, total, value = attend(None, 0, z)
+            for zz in range(nz - 2, -1, -1):
+                relay_loose(UP, zz)
             for copy in part_copies(below):
                 copy.wait_recv()
             side = jnp.transpose(jnp.broadcast_to(lin[0:1, :], (HD, rows)))[:, 0:1]
@@ -443,8 +449,8 @@
             finish_kv(KA)
             finish_kv(KB)
             loose(UP)
-            hub(UP, 0)
-            relay(UP, 0)
+            hub(UP, 0, 1, 2, 3)
+            relay(UP, 0, 1, 2, 3)
             relay_loose(UP, 0)
             step(WQ, 2, DOWN)
             step(WQ, 3, DOWN)
@@ -459,8 +465,6 @@
             relay_loose(DOWN, 2)
             relay_loose(DOWN, 3)
             take_kv(0)
-            hub(UP, 1, 2, 3)
-            relay(UP, 1, 2, 3)
             relay(DOWN, 2, 3)
             need_kv(0)
             state = attend(state, 0, 0)
@@ -501,8 +505,10 @@
             state = attend(state, 0, z)
             relay(UP, 0)
             relay_loose(UP, 1)
+            relay_loose(UP, 0)
             take_kv(0)
             need_kv(0)
+            relay(UP, 1)
             peak, total, value = attend(other, 1, 0)
             part[...] = (value / total).astype(jnp.bfloat16)
             lse[...] = jnp.transpose(
@@ -511,7 +517,6 @@
             for copy in part_copies(above):
                 go(copy)
             hub(UP, 1, 2, 3)
-            relay_loose(UP, 0)
             state = attend(state, 0, 0)
 
         hloc[...] = (state[2] / state[1]).astype(jnp.bfloat16)
@@ -524,11 +529,9 @@
                 relay_loose(DOWN, zz)
             relay(DOWN, 0, 1, 2, 3)
         elif top:
-            for zz in range(nz - 2, -1, -1):
-                relay_loose(UP, zz)
             relay(UP, 0, 1, 2, 3)
         elif z == 2:
-            relay(UP, 1, 2, 3)
+            relay(UP, 2, 3)
 
         @pl.when(t != z)
         def _():
@@ -536,6 +539,18 @@
             remote(ref, ref, wi_ss.at[z], wx_rs.at[nz], partner).wait_recv()
         for g in range(nt):
             wo_pass(g, c).start()
+        for g in range(nt):
+            wo_pass(g, 1 - c).wait_recv()
+        for k in range(1, nt):
+            g = (t + k) % nt
+            remote(hloc, head_cols(g), h_ss.at[k], h_rs.at[g], partner).wait_recv()
+        out_ref[...] = lax.dot_general(
+            hcat[...], wof[...], (((1,), (1,)), ((), ())), preferred_element_type=jnp.float32
+        ).astype(out_ref.dtype)
+        for k in range(1, nt):
+            head_copy(k).wait_send()
+        for g in range(nt):
+            wo_pass(g, c).wait_send()
         end_kv()
         for copy in sent:
             if isinstance(copy, tuple):
@@ -549,19 +564,6 @@
         @pl.when(plane_of == z)
         def _():
             plane(z)
-
-    for g in range(nt):
-        wo_pass(g, 1 - c).wait_recv()
-    for k in range(1, nt):
-        g = (t + k) % nt
-        remote(hloc, head_cols(g), h_ss.at[k], h_rs.at[g], partner).wait_recv()
-    out_ref[...] = lax.dot_general(
-        hcat[...], wof[...], (((1,), (1,)), ((), ())), preferred_element_type=jnp.float32
-    ).astype(out_ref.dtype)
-    for k in range(1, nt):
-        head_copy(k).wait_send()
-    for g in range(nt):
-        wo_pass(g, c).wait_send()
 
 
 def fused_body(nz, nt, hidden_states, resp_lengths, w_query, w_keyval, w_out):
@@ -579,7 +581,7 @@
             pltpu.VMEM((rows, depth), bf16),
             pltpu.VMEM((3, depth, HD), bf16),
             pltpu.VMEM((nout, HD), bf16),
-            pltpu.VMEM((nz, nout // 2, HD), bf16),
+            pltpu.VMEM((nz, nout * LOOSE // 8, HD), bf16),
             pltpu.VMEM((2 * nout, nt * HD), bf16),
             pltpu.VMEM((2, rows, HD), bf16),
             pltpu.VMEM((2, nz, 2 * rows, HD), bf16),

time: 45.7 us -> 43.1 us (0.943)
  Pallas kernels: 44.4 us -> 42.1 us
    pallas_call x1, Pallas kernels: 44.4 us -> 42.1 us  [fused_body(): pl.pallas_call(functools.partial(fused_kernel, nz, nt), out_shape=jax.Sha...]
where the time goes in v3:
time: 43.1 us; the launch traced here: 42.9 us
  Pallas kernels  42.1 us (98%)
  local copies, waits for them, and re-layouts  0.77 us (2%)
    pallas_call x1, Pallas kernels, fused_body(): pl.pallas_call(functools.partial(fused_kernel, nz, nt), out_shape=jax.Sha...  42.1 us

profile of v3, /device:TPU:25, one launch (start us, length us, event | category | flops | bytes accessed | tf_op | source)
XLA Modules:
  0.0 42.9 jit_solution(16515660984835502727)
XLA Ops:
  0.0 42.1 %shard_map.55 = bf16[256,896]{1,0:T(8,128)(2,1)S(1)} custom-call(s32[4]{0:T(128)} %lens_hbm.1, bf16[256,3584]{1,0:T(8,128)(2,1)} %hid_hbm.1, bf16[448,128]{1,0:T(8,128)(2,1)} %wq_hbm.1, bf16[448,256]{1,0:T(8,128)(2,1)} %wkv_hbm.1, bf16[448,128]{1,0:T(8,128)(2,1)} %bitcast.1), custom_call_target="tpu_custom_call" | custom-call | tf_op jit(solution)/shard_map/pallas_call | solution.py:575
  42.1 0.8 %copy.7 = bf16[256,896]{1,0:T(8,128)(2,1)} copy(bf16[256,896]{1,0:T(8,128)(2,1)S(1)} %shard_map.55) | data formatting | bytes 917504

commit v4 on v3

--- a/solution.py
+++ b/solution.py
@@ -83,6 +83,24 @@
     nout = wo_hbm.shape[0]
     own = pl.ds(pl.multiple_of(dp * shard, 64), shard)
 
+    barrier = pltpu.get_barrier_semaphore()
+    partner = {"dp": dp + 1 - 2 * c, "tp": t}
+    above, below = {"dp": dp + 2, "tp": t}, {"dp": dp - 2, "tp": t}
+    has_up, has_down = plane_of < nz - 1, plane_of > 0
+    pl.semaphore_signal(barrier, 1, device_id=partner, device_id_type=MESH)
+
+    @pl.when(has_up)
+    def _():
+        pl.semaphore_signal(barrier, 1, device_id=above, device_id_type=MESH)
+
+    @pl.when(has_down)
+    def _():
+        pl.semaphore_signal(barrier, 1, device_id=below, device_id_type=MESH)
+
+    for k in range(1, nt):
+        pl.semaphore_signal(
+            barrier, 1, device_id={"dp": dp, "tp": (t + k) % nt}, device_id_type=MESH
+        )
     loads = [
         pltpu.make_async_copy(wkv_hbm.at[:, pl.ds(0, HD)], w.at[KA, own], loc_sem.at[KA]),
         pltpu.make_async_copy(wkv_hbm.at[:, pl.ds(HD, HD)], w.at[KB, own], loc_sem.at[KB]),
@@ -94,24 +112,6 @@
     for load in loads:
         load.start()
 
-    barrier = pltpu.get_barrier_semaphore()
-    partner = {"dp": dp + 1 - 2 * c, "tp": t}
-    above, below = {"dp": dp + 2, "tp": t}, {"dp": dp - 2, "tp": t}
-    has_up, has_down = plane_of < nz - 1, plane_of > 0
-    pl.semaphore_signal(barrier, 1, device_id=partner, device_id_type=MESH)
-
-    @pl.when(has_up)
-    def _():
-        pl.semaphore_signal(barrier, 1, device_id=above, device_id_type=MESH)
-
-    @pl.when(has_down)
-    def _():
-        pl.semaphore_signal(barrier, 1, device_id=below, device_id_type=MESH)
-
-    for k in range(1, nt):
-        pl.semaphore_signal(
-            barrier, 1, device_id={"dp": dp, "tp": (t + k) % nt}, device_id_type=MESH
-        )
     pl.semaphore_wait(barrier, nt + has_up.astype(jnp.int32) + has_down.astype(jnp.int32))
 
     def chunk(item, zz, cc):
@@ -125,7 +125,9 @@
     def chain(item, zz, way):
         ref = chunk(item, zz, c)
         recv = prs.at[item, zz] if way == SIDE else rs.at[item, zz]
-        return remote(ref, ref, ss.at[item, zz, way], recv, (above, below, partner)[way])
+        return remote(
+            ref, ref, ss.at[int(item == WQ), way], recv, (above, below, partner)[way]
+        )
 
     def device(zz, tt):
         return {"dp": 2 * zz + c, "tp": tt}
@@ -136,17 +138,20 @@
     def kv_copy(z, b, zz):
         role = t // (nt // 2)
         return remote(
-            kvloc.at[b], kvb.at[role, z, half_rows], kv_ss.at[b, zz], kv_rs.at[role, z],
+            kvloc.at[b], kvb.at[role, z, half_rows], kv_ss.at[int(zz == z)], kv_rs.at[z],
             device(zz, 2 * (t % (nt // 2)) + b),
         )
 
+    def kv_over(z, b):
+        role = t // (nt // 2)
+        return remote(
+            kvloc.at[b], kvb.at[role, z, pl.ds(0, rows)], kp_ss.at[0], kp_rs.at[z],
+            {"dp": dp + 1, "tp": 2 * (t % (nt // 2)) + b},
+        )
+
     def kv_pass(z, role):
         ref = kvb.at[role, z, half_rows]
-        return remote(ref, ref, kp_ss.at[role, z], kp_rs.at[role, z], partner)
-
-    def kv_passed(z, role):
-        ref = kvb.at[role, z, other_rows]
-        return remote(ref, ref, kp_ss.at[role, z], kp_rs.at[role, z], partner)
+        return remote(ref, ref, kp_ss.at[0], kp_rs.at[z], partner)
 
     def wo_block(g, cc):
         return wof.at[
@@ -165,29 +170,30 @@
 
     def wo_chain(g, way):
         ref = wo_ref(g, way)
-        return remote(ref, ref, wc_ss.at[g, way], wi_rs.at[g], (above, below)[way])
+        full = int(g != (nt - 1 if way == UP else 0))
+        return remote(ref, ref, wc_ss.at[full, way], wi_rs.at[g], (above, below)[way])
 
     def wo_loose(src, zz, way):
-        return remote(src, wox.at[zz], wx_ss.at[zz, way], wx_rs.at[zz], (above, below)[way])
+        return remote(src, wox.at[zz], wx_ss.at[way], wx_rs.at[zz], (above, below)[way])
 
     def wo_cross(zz):
-        return remote(woc, wo_block(t, c), wi_ss.at[zz], wi_rs.at[t], {"dp": dp, "tp": zz})
+        return remote(woc, wo_block(t, c), wi_ss.at[0], wi_rs.at[t], {"dp": dp, "tp": zz})
 
     def wo_loose_cross(zz):
         return remote(
-            wox.at[zz], wo_half(t, 1), wi_ss.at[zz], wx_rs.at[nz], {"dp": dp, "tp": zz}
+            wox.at[zz], wo_half(t, 1), wi_ss.at[1], wx_rs.at[nz], {"dp": dp, "tp": zz}
         )
 
     def wo_pass(g, cc):
         ref = wo_block(g, cc)
-        return remote(ref, ref, wp_ss.at[g], wp_rs.at[g], partner)
+        return remote(ref, ref, wp_ss.at[0], wp_rs.at[0], partner)
 
     def head_cols(g):
         return hcat.at[:, pl.ds(pl.multiple_of(g * HD, HD), HD)]
 
     def head_copy(k):
         return remote(
-            hloc, head_cols(t), h_ss.at[k], h_rs.at[t], {"dp": dp, "tp": (t + k) % nt}
+            hloc, head_cols(t), h_ss.at[0], h_rs.at[0], {"dp": dp, "tp": (t + k) % nt}
         )
 
     loads[5].wait()
@@ -198,28 +204,41 @@
         ends.append(end)
 
     def plane(z):
-        sent = []
+        counts = {}
         seen = set()
         top, bottom = z == nz - 1, z == 0
         kv_to = [zz for zz in (nz - 2, nz - 3, 0) if zz >= z] if not top else [z]
         span = 2 * shard
 
-        def go(copy):
+        def tally(key, rows_sent, cond=None):
+            counts[key] = (counts.get(key, (0, cond))[0] + rows_sent, cond)
+
+        def go(copy, key, rows_sent):
             copy.start()
-            sent.append(copy)
+            tally(key, rows_sent)
+
+        def go_chain(item, zz, way):
+            go(chain(item, zz, way), ("w", int(item == WQ), way), shard)
+
+        def received(ref, sem):
+            remote(ref, ref, sem, sem, partner).wait_recv()
+
+        def drain(sem, amount):
+            ref = w.at[0, pl.ds(0, amount)]
+            remote(ref, ref, sem, sem, partner).wait_send()
 
         def own_send(item, way):
-            go(chain(item, z, way))
+            go_chain(item, z, way)
 
         def event(item, zz, *ways):
             ref = chunk(item, zz, c)
-            remote(ref, ref, ss.at[item, zz, UP], rs.at[item, zz], partner).wait_recv()
+            received(ref, rs.at[item, zz])
             for way in ways + (SIDE,):
-                go(chain(item, zz, way))
+                go_chain(item, zz, way)
 
         def dot(item, zz):
             ref = chunk(item, zz, 1 - c)
-            remote(ref, ref, ss.at[item, zz, SIDE], prs.at[item, zz], partner).wait_recv()
+            received(ref, prs.at[item, zz])
             part_sum = jnp.dot(
                 hid[:, zz * span:(zz + 1) * span], w[item, zz * span:(zz + 1) * span, :],
                 preferred_element_type=jnp.float32,
@@ -230,45 +249,63 @@
                 seen.add(item)
                 acc[item] = part_sum
 
-        def finish_kv(b):
-            kvloc[b] = acc[b].astype(jnp.bfloat16)
+        def finish_kv(*picks):
             role = t // (nt // 2)
+            for b in picks:
+                kvloc[b] = acc[b].astype(jnp.bfloat16)
             for zz in kv_to:
                 if zz != z:
-                    go(kv_copy(z, b, zz))
-            mine = 2 * (t % (nt // 2)) + b == t
-
-            @pl.when(jnp.logical_not(mine))
+                    for b in picks:
+                        go(kv_copy(z, b, zz), ("far",), rows)
+            for b in picks:
+                mine = 2 * (t % (nt // 2)) + b == t
+                if top:
+                    go_if(c == 0, kv_over(z, b), ("pass",), rows)
+
+                @pl.when(jnp.logical_not(mine))
+                def _():
+                    kv_copy(z, b, z).start()
+
+                @pl.when(mine)
+                def _():
+                    kvb[role, z, half_rows, :] = kvloc[b]
+
+        k_here, v_here = t // 2 == t, t // 2 + nt // 2 == t
+        none_here = jnp.logical_not(jnp.logical_or(k_here, v_here))
+
+        def end_kv():
+            @pl.when(none_here)
             def _():
-                kv_copy(z, b, z).start()
-
-            @pl.when(mine)
+                drain(kv_ss.at[1], 2 * rows)
+
+            @pl.when(jnp.logical_not(none_here))
             def _():
-                kvb[role, z, half_rows, :] = kvloc[b]
-
-        def end_kv():
-            for b in range(2):
-                @pl.when(2 * (t % (nt // 2)) + b != t)
-                def _():
-                    kv_copy(z, b, z).wait_send()
+                drain(kv_ss.at[1], rows)
 
         def take_kv(zs):
-            for role in range(2):
-                arrived = remote(
-                    kvloc.at[0], kvb.at[role, zs, half_rows], kv_ss.at[0, zs],
-                    kv_rs.at[role, zs], partner,
-                )
-                if zs == z:
-                    @pl.when(t // 2 + role * (nt // 2) != t)
-                    def _():
-                        arrived.wait_recv()
-                else:
-                    arrived.wait_recv()
-                go(kv_pass(zs, role))
+            both = kvb.at[:, zs, half_rows]
+            if zs == z:
+                @pl.when(none_here)
+                def _():
+                    received(both, kv_rs.at[zs])
+
+                @pl.when(jnp.logical_not(none_here))
+                def _():
+                    received(kvb.at[jnp.where(k_here, 1, 0), zs, half_rows], kv_rs.at[zs])
+            else:
+                received(both, kv_rs.at[zs])
+            if not top:
+                for role in range(2):
+                    go(kv_pass(zs, role), ("pass",), rows)
 
         def need_kv(zs):
-            for role in range(2):
-                kv_passed(zs, role).wait_recv()
+            both = kvb.at[:, zs, other_rows]
+            if top:
+                @pl.when(c == 1)
+                def _():
+                    received(both, kp_rs.at[zs])
+            else:
+                received(both, kp_rs.at[zs])
 
         def finish_q():
             qb[0] = (acc[WQ] * (HD ** -0.5)).astype(jnp.bfloat16)
@@ -299,14 +336,14 @@
 
         last = nt - 1
 
-        def go_if(cond, copy):
+        def go_if(cond, copy, key, rows_sent):
             @pl.when(cond)
             def _():
                 copy.start()
-            sent.append((cond, copy))
+            tally(key, rows_sent, cond)
 
         def wo_arrived(g, ref):
-            remote(ref, ref, wc_ss.at[g, UP], wi_rs.at[g], partner).wait_recv()
+            received(ref, wi_rs.at[g])
 
         def collect():
             @pl.when(t == z)
@@ -314,37 +351,46 @@
                 for g in range(nt):
                     if g != z:
                         wo_arrived(g, wo_block(g, c))
+                    wo_pass(g, c).start()
 
         def hub(way, *picks):
             for k in picks:
-                go_if(t == z, wo_chain(k if way == UP else (k + 1) % nt, way))
+                @pl.when(t == z)
+                def _():
+                    wo_chain(k if way == UP else (k + 1) % nt, way).start()
 
         def loose(way):
-            go_if(t == (last if way == UP else 0), wo_loose(woc.at[pl.ds(split, nout - split)], z, way))
-
-        def relay(way, *picks):
+            go_if(
+                t == (last if way == UP else 0),
+                wo_loose(woc.at[pl.ds(split, nout - split)], z, way), ("x", way), nout - split,
+            )
+
+        def relay(way, *picks, only=None):
             if z == (0 if way == UP else nz - 1):
                 return
             mine = t < z if way == UP else t > z
+            if only is not None:
+                mine = t == only
             for k in picks:
                 g = k if way == UP else (k + 1) % nt
 
                 @pl.when(mine)
                 def _():
                     wo_arrived(g, wo_ref(g, way))
-                if z != (nz - 1 if way == UP else 0):
-                    go_if(mine, wo_chain(g, way))
+                    if z != (nz - 1 if way == UP else 0):
+                        wo_chain(g, way).start()
+                    if k < nt - 1:
+                        wo_pass(g, c).start()
 
         def relay_loose(way, zs):
             mine = t == (last if way == UP else 0)
 
             @pl.when(mine)
             def _():
-                ref = wox.at[zs]
-                remote(ref, ref, wx_ss.at[zs, way], wx_rs.at[zs], partner).wait_recv()
+                received(wox.at[zs], wx_rs.at[zs])
             if z != (nz - 1 if way == UP else 0):
-                go_if(mine, wo_loose(wox.at[zs], zs, way))
-            go_if(mine, wo_loose_cross(zs))
+                go_if(mine, wo_loose(wox.at[zs], zs, way), ("x", way), nout - split)
+            go_if(mine, wo_loose_cross(zs), ("cross", way), nout - split)
 
         def query_copy():
             return remote(qb.at[0], qb.at[1], pt_ss.at[0], pt_rs.at[0], below)
@@ -364,13 +410,18 @@
                 own_send(item, DOWN)
             own_send(item, SIDE)
         loads[4].wait()
-        go_if(t != z, wo_cross(z))
+        go_if(t != z, wo_cross(z), ("own",), nout)
 
         @pl.when(t == z)
         def _():
             wo_block(t, c)[...] = woc[...]
 
         loads[3].wait()
+
+        if top:
+            @pl.when(c == 0)
+            def _():
+                kvb[:, z, rows:, :] = jnp.zeros((2, rows, HD), kvb.dtype)
 
         waiting = [(WQ, z), (KA, z), (KB, z)]
 
@@ -393,8 +444,7 @@
                 step(KA, zz)
                 step(KB, zz)
             settle(0)
-            finish_kv(KA)
-            finish_kv(KB)
+            finish_kv(KA, KB)
             for zz in range(1, nz):
                 step(WQ, zz, keep=1)
             take_kv(z)
@@ -413,7 +463,7 @@
             step(WQ, 0)
             settle(0)
             finish_q()
-            go(query_copy())
+            go(query_copy(), ("query",), rows)
             step(KA, 1, keep=1)
             step(KB, 1, keep=1)
             step(KA, 0, keep=1)
@@ -446,8 +496,7 @@
             own_send(WQ, DOWN)
             collect()
             settle(0)
-            finish_kv(KA)
-            finish_kv(KB)
+            finish_kv(KA, KB)
             loose(UP)
             hub(UP, 0, 1, 2, 3)
             relay(UP, 0, 1, 2, 3)
@@ -477,7 +526,7 @@
             step(KA, 1)
             step(WQ, 3, DOWN)
             step(WQ, 0, UP)
-            go(chain(KA, 1, UP))
+            go_chain(KA, 1, UP)
             collect()
             loose(DOWN)
             hub(DOWN, 0, 1, 2, 3)
@@ -490,8 +539,7 @@
             loose(UP)
             hub(UP, 0)
             settle(0)
-            finish_kv(KA)
-            finish_kv(KB)
+            finish_kv(KA, KB)
             finish_q()
             relay(DOWN, 2, 3)
             take_kv(1)
@@ -503,21 +551,22 @@
             need_kv(z)
             other = attend(other, 1, z)
             state = attend(state, 0, z)
-            relay(UP, 0)
+            relay(UP, 0, only=1)
             relay_loose(UP, 1)
             relay_loose(UP, 0)
             take_kv(0)
             need_kv(0)
-            relay(UP, 1)
             peak, total, value = attend(other, 1, 0)
             part[...] = (value / total).astype(jnp.bfloat16)
             lse[...] = jnp.transpose(
                 jnp.broadcast_to(peak + jnp.log(total), (rows, HD))
             )[:lse.shape[0], :]
             for copy in part_copies(above):
-                go(copy)
+                copy.start()
             hub(UP, 1, 2, 3)
+            relay(UP, 0, only=0)
             state = attend(state, 0, 0)
+            relay(UP, 1)
 
         hloc[...] = (state[2] / state[1]).astype(jnp.bfloat16)
         for k in range(1, nt):
@@ -535,30 +584,45 @@
 
         @pl.when(t != z)
         def _():
-            ref = wox.at[0]
-            remote(ref, ref, wi_ss.at[z], wx_rs.at[nz], partner).wait_recv()
-        for g in range(nt):
-            wo_pass(g, c).start()
-        for g in range(nt):
-            wo_pass(g, 1 - c).wait_recv()
-        for k in range(1, nt):
-            g = (t + k) % nt
-            remote(hloc, head_cols(g), h_ss.at[k], h_rs.at[g], partner).wait_recv()
+            received(wox.at[0], wx_rs.at[nz])
+
+        @pl.when(t < z)
+        def _():
+            wo_pass(last, c).start()
+
+        @pl.when(t > z)
+        def _():
+            wo_pass(0, c).start()
+        received(wof.at[pl.ds(pl.multiple_of((1 - c) * nout, 64), nout)], wp_rs.at[0])
+        received(hid.at[:, pl.ds(0, (nt - 1) * HD)], h_rs.at[0])
         out_ref[...] = lax.dot_general(
             hcat[...], wof[...], (((1,), (1,)), ((), ())), preferred_element_type=jnp.float32
         ).astype(out_ref.dtype)
-        for k in range(1, nt):
-            head_copy(k).wait_send()
-        for g in range(nt):
-            wo_pass(g, c).wait_send()
+        drain(h_ss.at[0], (nt - 1) * rows)
+        drain(wp_ss.at[0], nt * nout)
         end_kv()
-        for copy in sent:
-            if isinstance(copy, tuple):
-                @pl.when(copy[0])
-                def _():
-                    copy[1].wait_send()
+        if z == nz - 2:
+            for copy in part_copies(above):
+                copy.wait_send()
+        for way, ends_here, mine in ((UP, top, t <= z), (DOWN, bottom, t >= z)):
+            if not ends_here:
+                @pl.when(mine)
+                def _():
+                    drain(wc_ss.at[1, way], (nt - 1) * nout)
+                    drain(wc_ss.at[0, way], split)
+        for key, (amount, cond) in counts.items():
+            sem = {
+                "w": lambda: ss.at[key[1], key[2]], "far": lambda: kv_ss.at[0],
+                "pass": lambda: kp_ss.at[0], "x": lambda: wx_ss.at[key[1]],
+                "cross": lambda: wi_ss.at[1], "own": lambda: wi_ss.at[0],
+                "query": lambda: pt_ss.at[0],
+            }[key[0]]()
+            if cond is None:
+                drain(sem, amount)
             else:
-                copy.wait_send()
+                @pl.when(cond)
+                def _():
+                    drain(sem, amount)
 
     for z in range(nz):
         @pl.when(plane_of == z)
@@ -594,24 +658,24 @@
             pltpu.VMEM((rows, HD), bf16),
             pltpu.VMEM((rows, nt * HD), bf16),
             dma((6,)),
-            dma((3, nz, 3)),
+            dma((2, 3)),
             dma((3, nz)),
             dma((3, nz)),
-            dma((2, nz)),
-            dma((2, nz)),
-            dma((2, nz)),
-            dma((2, nz)),
-            dma((nt, 2)),
-            dma((nz, 2)),
+            dma((2,)),
+            dma((nz,)),
+            dma((1,)),
+            dma((nz,)),
+            dma((2, 2)),
+            dma((2,)),
             dma((nz + 1,)),
-            dma((nz,)),
+            dma((2,)),
             dma((nt,)),
-            dma((nt,)),
-            dma((nt,)),
+            dma((1,)),
+            dma((1,)),
             dma((3,)),
             dma((3,)),
-            dma((nt,)),
-            dma((nt,)),
+            dma((1,)),
+            dma((1,)),
             pltpu.SMEM(resp_lengths.shape, jnp.int32),
         ],
         compiler_params=pltpu.CompilerParams(

time: 43.1 us -> 41.7 us (0.968)
  Pallas kernels: 42.1 us -> 40.7 us
    pallas_call x1, Pallas kernels: 42.1 us -> 40.7 us  [fused_body(): pl.pallas_call(functools.partial(fused_kernel, nz, nt), out_shape=jax.Sha...]
where the time goes in v4:
time: 41.7 us; the launch traced here: 41.5 us
  Pallas kernels  40.7 us (98%)
  local copies, waits for them, and re-layouts  0.77 us (2%)
    pallas_call x1, Pallas kernels, fused_body(): pl.pallas_call(functools.partial(fused_kernel, nz, nt), out_shape=jax.Sha...  40.7 us

profile of v4, /device:TPU:25, one launch (start us, length us, event | category | flops | bytes accessed | tf_op | source)
XLA Modules:
  0.0 41.5 jit_solution(1506856163832442390)
XLA Ops:
  0.0 40.7 %shard_map.55 = bf16[256,896]{1,0:T(8,128)(2,1)S(1)} custom-call(s32[4]{0:T(128)} %lens_hbm.1, bf16[256,3584]{1,0:T(8,128)(2,1)} %hid_hbm.1, bf16[448,128]{1,0:T(8,128)(2,1)} %wq_hbm.1, bf16[448,256]{1,0:T(8,128)(2,1)} %wkv_hbm.1, bf16[448,128]{1,0:T(8,128)(2,1)} %bitcast.1), custom_call_target="tpu_custom_call" | custom-call | tf_op jit(solution)/shard_map/pallas_call | solution.py:639
  40.7 0.8 %copy.7 = bf16[256,896]{1,0:T(8,128)(2,1)} copy(bf16[256,896]{1,0:T(8,128)(2,1)S(1)} %shard_map.55) | data formatting | bytes 917504

commit v5 on v4

--- a/solution.py
+++ b/solution.py
@@ -66,7 +66,7 @@
 KA, KB, WQ = range(3)
 UP, DOWN, SIDE = range(3)
 NEG = -1e30
-LOOSE = 6
+LOOSE = ((28, 28, 12, 0), (0, 12, 24, 18))
 
 
 def fused_kernel(
@@ -158,30 +158,41 @@
             pl.ds(pl.multiple_of(cc * nout, 64), nout), pl.ds(pl.multiple_of(g * HD, HD), HD)
         ]
 
-    split = nout - wox.shape[1]
-
-    def wo_half(g, h):
+    def loose_rows(zs, way):
+        return nout * LOOSE[way][zs] // 512 * 16
+
+    def wo_half(g, h, zs, way):
+        split = nout - loose_rows(zs, way)
         start = pl.multiple_of(c * nout + h * split, 16)
         size = nout - split if h else split
         return wof.at[pl.ds(start, size), pl.ds(pl.multiple_of(g * HD, HD), HD)]
 
-    def wo_ref(g, way):
-        return wo_half(g, 0) if g == (nt - 1 if way == UP else 0) else wo_block(g, c)
-
-    def wo_chain(g, way):
-        ref = wo_ref(g, way)
-        full = int(g != (nt - 1 if way == UP else 0))
+    def loose_block(way):
+        return nt - 1 if way == UP else 0
+
+    def wo_chain(g, way, zs):
+        full = int(g != loose_block(way))
+        ref = wo_block(g, c) if full else wo_half(g, 0, zs, way)
         return remote(ref, ref, wc_ss.at[full, way], wi_rs.at[g], (above, below)[way])
 
+    def wo_twin(way, zs):
+        ref = wo_half(loose_block(way), 0, zs, way)
+        to = {"dp": dp + (2 if way == UP else -2) + 1 - 2 * c, "tp": t}
+        return remote(ref, ref, wc_ss.at[0, way], wp_rs.at[0], to)
+
     def wo_loose(src, zz, way):
-        return remote(src, wox.at[zz], wx_ss.at[way], wx_rs.at[zz], (above, below)[way])
+        return remote(
+            src, wox.at[zz, pl.ds(0, loose_rows(zz, way))], wx_ss.at[way], wx_rs.at[zz],
+            (above, below)[way],
+        )
 
     def wo_cross(zz):
         return remote(woc, wo_block(t, c), wi_ss.at[0], wi_rs.at[t], {"dp": dp, "tp": zz})
 
-    def wo_loose_cross(zz):
+    def wo_loose_cross(zz, way):
         return remote(
-            wox.at[zz], wo_half(t, 1), wi_ss.at[1], wx_rs.at[nz], {"dp": dp, "tp": zz}
+            wox.at[zz, pl.ds(0, loose_rows(zz, way))], wo_half(t, 1, zz, way), wi_ss.at[1],
+            wx_rs.at[nz], {"dp": dp, "tp": zz},
         )
 
     def wo_pass(g, cc):
@@ -353,44 +364,63 @@
                         wo_arrived(g, wo_block(g, c))
                     wo_pass(g, c).start()
 
+        def last_hop(way):
+            return z == (nz - 2 if way == UP else 1)
+
+        def send_on(g, way, zs):
+            wo_chain(g, way, zs).start()
+            if g == loose_block(way) and last_hop(way):
+                wo_twin(way, zs).start()
+
         def hub(way, *picks):
             for k in picks:
                 @pl.when(t == z)
                 def _():
-                    wo_chain(k if way == UP else (k + 1) % nt, way).start()
+                    send_on(k if way == UP else (k + 1) % nt, way, z)
 
         def loose(way):
+            size = loose_rows(z, way)
             go_if(
                 t == (last if way == UP else 0),
-                wo_loose(woc.at[pl.ds(split, nout - split)], z, way), ("x", way), nout - split,
+                wo_loose(woc.at[pl.ds(nout - size, size)], z, way), ("x", way), size,
             )
 
         def relay(way, *picks, only=None):
             if z == (0 if way == UP else nz - 1):
                 return
+            ends = z == (nz - 1 if way == UP else 0)
             mine = t < z if way == UP else t > z
             if only is not None:
                 mine = t == only
             for k in picks:
                 g = k if way == UP else (k + 1) % nt
-
-                @pl.when(mine)
-                def _():
-                    wo_arrived(g, wo_ref(g, way))
-                    if z != (nz - 1 if way == UP else 0):
-                        wo_chain(g, way).start()
-                    if k < nt - 1:
+                if k < nt - 1:
+                    @pl.when(mine)
+                    def _():
+                        wo_arrived(g, wo_block(g, c))
+                        if not ends:
+                            send_on(g, way, None)
                         wo_pass(g, c).start()
+                else:
+                    for zs in range(z) if way == UP else range(z + 1, nz):
+                        @pl.when(t == zs)
+                        def _():
+                            wo_arrived(g, wo_half(g, 0, zs, way))
+                            if not ends:
+                                send_on(g, way, zs)
 
         def relay_loose(way, zs):
             mine = t == (last if way == UP else 0)
+            size = loose_rows(zs, way)
 
             @pl.when(mine)
             def _():
-                received(wox.at[zs], wx_rs.at[zs])
+                received(wox.at[zs, pl.ds(0, size)], wx_rs.at[zs])
             if z != (nz - 1 if way == UP else 0):
-                go_if(mine, wo_loose(wox.at[zs], zs, way), ("x", way), nout - split)
-            go_if(mine, wo_loose_cross(zs), ("cross", way), nout - split)
+                go_if(
+                    mine, wo_loose(wox.at[zs, pl.ds(0, size)], zs, way), ("x", way), size
+                )
+            go_if(mine, wo_loose_cross(zs, way), ("cross", way), size)
 
         def query_copy():
             return remote(qb.at[0], qb.at[1], pt_ss.at[0], pt_rs.at[0], below)
@@ -582,24 +612,33 @@
         elif z == 2:
             relay(UP, 2, 3)
 
-        @pl.when(t != z)
-        def _():
-            received(wox.at[0], wx_rs.at[nz])
-
-        @pl.when(t < z)
-        def _():
-            wo_pass(last, c).start()
-
-        @pl.when(t > z)
-        def _():
-            wo_pass(0, c).start()
+        for zs in range(nz):
+            if zs != z:
+                way = UP if zs < z else DOWN
+                g = loose_block(way)
+
+                @pl.when(t == zs)
+                def _():
+                    late = wo_half(g, 1, zs, way)
+                    received(late, wx_rs.at[nz])
+                    if top or bottom:
+                        remote(late, late, wp_ss.at[0], wp_rs.at[0], partner).start()
+                    else:
+                        wo_pass(g, c).start()
         received(wof.at[pl.ds(pl.multiple_of((1 - c) * nout, 64), nout)], wp_rs.at[0])
         received(hid.at[:, pl.ds(0, (nt - 1) * HD)], h_rs.at[0])
         out_ref[...] = lax.dot_general(
             hcat[...], wof[...], (((1,), (1,)), ((), ())), preferred_element_type=jnp.float32
         ).astype(out_ref.dtype)
         drain(h_ss.at[0], (nt - 1) * rows)
-        drain(wp_ss.at[0], nt * nout)
+        drain(wp_ss.at[0], (nt - 1) * nout)
+        for zs in range(nz):
+            way = UP if zs < z else DOWN
+            part_only = zs != z and (top or bottom)
+
+            @pl.when(t == zs)
+            def _():
+                drain(wp_ss.at[0], loose_rows(zs, way) if part_only else nout)
         end_kv()
         if z == nz - 2:
             for copy in part_copies(above):
@@ -609,7 +648,11 @@
                 @pl.when(mine)
                 def _():
                     drain(wc_ss.at[1, way], (nt - 1) * nout)
-                    drain(wc_ss.at[0, way], split)
+                for zs in range(z + 1) if way == UP else range(z, nz):
+                    @pl.when(t == zs)
+                    def _():
+                        rest = nout - loose_rows(zs, way)
+                        drain(wc_ss.at[0, way], rest * (2 if last_hop(way) else 1))
         for key, (amount, cond) in counts.items():
             sem = {
                 "w": lambda: ss.at[key[1], key[2]], "far": lambda: kv_ss.at[0],
@@ -645,7 +688,7 @@
             pltpu.VMEM((rows, depth), bf16),
             pltpu.VMEM((3, depth, HD), bf16),
             pltpu.VMEM((nout, HD), bf16),
-            pltpu.VMEM((nz, nout * LOOSE // 8, HD), bf16),
+            pltpu.VMEM((nz, nout, HD), bf16),
             pltpu.VMEM((2 * nout, nt * HD), bf16),
             pltpu.VMEM((2, rows, HD), bf16),
             pltpu.VMEM((2, nz, 2 * rows, HD), bf16),

time: 41.7 us -> 41.4 us (level)
  no operation moved by 1% of the time
where the time goes in v5:
time: 41.4 us; the launch traced here: 41.3 us
  Pallas kernels  40.5 us (98%)
  local copies, waits for them, and re-layouts  0.77 us (2%)
    pallas_call x1, Pallas kernels, fused_body(): pl.pallas_call(functools.partial(fused_kernel, nz, nt), out_shape=jax.Sha...  40.5 us

profile of v5, /device:TPU:25, one launch (start us, length us, event | category | flops | bytes accessed | tf_op | source)
XLA Modules:
  0.0 41.3 jit_solution(11972338348992003100)
XLA Ops:
  0.0 40.5 %shard_map.55 = bf16[256,896]{1,0:T(8,128)(2,1)S(1)} custom-call(s32[4]{0:T(128)} %lens_hbm.1, bf16[256,3584]{1,0:T(8,128)(2,1)} %hid_hbm.1, bf16[448,128]{1,0:T(8,128)(2,1)} %wq_hbm.1, bf16[448,256]{1,0:T(8,128)(2,1)} %wkv_hbm.1, bf16[448,128]{1,0:T(8,128)(2,1)} %bitcast.1), custom_call_target="tpu_custom_call" | custom-call | tf_op jit(solution)/shard_map/pallas_call | solution.py:682
  40.5 0.8 %copy.7 = bf16[256,896]{1,0:T(8,128)(2,1)} copy(bf16[256,896]{1,0:T(8,128)(2,1)S(1)} %shard_map.55) | data formatting | bytes 917504

commit v6 on v5

--- a/solution.py
+++ b/solution.py
@@ -170,10 +170,14 @@
     def loose_block(way):
         return nt - 1 if way == UP else 0
 
-    def wo_chain(g, way, zs):
+    def wo_piece(g, h):
+        start = pl.multiple_of(c * nout + h * (nout // 2), 16)
+        return wof.at[pl.ds(start, nout // 2), pl.ds(pl.multiple_of(g * HD, HD), HD)]
+
+    def wo_chain(g, way, zs, h=0):
         full = int(g != loose_block(way))
-        ref = wo_block(g, c) if full else wo_half(g, 0, zs, way)
-        return remote(ref, ref, wc_ss.at[full, way], wi_rs.at[g], (above, below)[way])
+        ref = wo_piece(g, h) if full else wo_half(g, 0, zs, way)
+        return remote(ref, ref, wc_ss.at[full, way], wi_rs.at[g, h], (above, below)[way])
 
     def wo_twin(way, zs):
         ref = wo_half(loose_block(way), 0, zs, way)
@@ -187,7 +191,7 @@
         )
 
     def wo_cross(zz):
-        return remote(woc, wo_block(t, c), wi_ss.at[0], wi_rs.at[t], {"dp": dp, "tp": zz})
+        return remote(woc, wo_block(t, c), wi_ss.at[0], wi_rs.at[t, 0], {"dp": dp, "tp": zz})
 
     def wo_loose_cross(zz, way):
         return remote(
@@ -353,8 +357,8 @@
                 copy.start()
             tally(key, rows_sent, cond)
 
-        def wo_arrived(g, ref):
-            received(ref, wi_rs.at[g])
+        def wo_arrived(g, ref, h=0):
+            received(ref, wi_rs.at[g, h])
 
         def collect():
             @pl.when(t == z)
@@ -368,8 +372,12 @@
             return z == (nz - 2 if way == UP else 1)
 
         def send_on(g, way, zs):
+            if g != loose_block(way):
+                for h in range(2):
+                    wo_chain(g, way, zs, h).start()
+                return
             wo_chain(g, way, zs).start()
-            if g == loose_block(way) and last_hop(way):
+            if last_hop(way):
                 wo_twin(way, zs).start()
 
         def hub(way, *picks):
@@ -385,7 +393,7 @@
                 wo_loose(woc.at[pl.ds(nout - size, size)], z, way), ("x", way), size,
             )
 
-        def relay(way, *picks, only=None):
+        def relay(way, *picks, only=None, halves=(0, 1)):
             if z == (0 if way == UP else nz - 1):
                 return
             ends = z == (nz - 1 if way == UP else 0)
@@ -397,10 +405,12 @@
                 if k < nt - 1:
                     @pl.when(mine)
                     def _():
-                        wo_arrived(g, wo_block(g, c))
-                        if not ends:
-                            send_on(g, way, None)
-                        wo_pass(g, c).start()
+                        for h in halves:
+                            wo_arrived(g, wo_piece(g, h), h)
+                            if not ends:
+                                wo_chain(g, way, None, h).start()
+                        if halves[-1] == 1:
+                            wo_pass(g, c).start()
                 else:
                     for zs in range(z) if way == UP else range(z + 1, nz):
                         @pl.when(t == zs)
@@ -586,6 +596,7 @@
             relay_loose(UP, 0)
             take_kv(0)
             need_kv(0)
+            relay(UP, 0, only=0, halves=(0,))
             peak, total, value = attend(other, 1, 0)
             part[...] = (value / total).astype(jnp.bfloat16)
             lse[...] = jnp.transpose(
@@ -594,9 +605,10 @@
             for copy in part_copies(above):
                 copy.start()
             hub(UP, 1, 2, 3)
-            relay(UP, 0, only=0)
+            relay(UP, 0, only=0, halves=(1,))
+            relay(UP, 1, halves=(0,))
             state = attend(state, 0, 0)
-            relay(UP, 1)
+            relay(UP, 1, halves=(1,))
 
         hloc[...] = (state[2] / state[1]).astype(jnp.bfloat16)
         for k in range(1, nt):
@@ -712,7 +724,7 @@
             dma((2,)),
             dma((nz + 1,)),
             dma((2,)),
-            dma((nt,)),
+            dma((nt, 2)),
             dma((1,)),
             dma((1,)),
             dma((3,)),

time: 41.4 us -> 41 us (level)
  no operation moved by 1% of the time
where the time goes in v6:
time: 41 us; the launch traced here: 40.9 us
  Pallas kernels  40.1 us (98%)
  local copies, waits for them, and re-layouts  0.77 us (2%)
    pallas_call x1, Pallas kernels, fused_body(): pl.pallas_call(functools.partial(fused_kernel, nz, nt), out_shape=jax.Sha...  40.1 us

profile of v6, /device:TPU:25, one launch (start us, length us, event | category | flops | bytes accessed | tf_op | source)
XLA Modules:
  0.0 40.9 jit_solution(14543368083736917306)
XLA Ops:
  0.0 40.1 %shard_map.55 = bf16[256,896]{1,0:T(8,128)(2,1)S(1)} custom-call(s32[4]{0:T(128)} %lens_hbm.1, bf16[256,3584]{1,0:T(8,128)(2,1)} %hid_hbm.1, bf16[448,128]{1,0:T(8,128)(2,1)} %wq_hbm.1, bf16[448,256]{1,0:T(8,128)(2,1)} %wkv_hbm.1, bf16[448,128]{1,0:T(8,128)(2,1)} %bitcast.1), custom_call_target="tpu_custom_call" | custom-call | tf_op jit(solution)/shard_map/pallas_call | solution.py:694
  40.1 0.8 %copy.7 = bf16[256,896]{1,0:T(8,128)(2,1)} copy(bf16[256,896]{1,0:T(8,128)(2,1)S(1)} %shard_map.55) | data formatting | bytes 917504

commit v7 on v6

--- a/solution.py
+++ b/solution.py
@@ -606,9 +606,8 @@
                 copy.start()
             hub(UP, 1, 2, 3)
             relay(UP, 0, only=0, halves=(1,))
-            relay(UP, 1, halves=(0,))
+            relay(UP, 1)
             state = attend(state, 0, 0)
-            relay(UP, 1, halves=(1,))
 
         hloc[...] = (state[2] / state[1]).astype(jnp.bfloat16)
         for k in range(1, nt):

time: 41 us -> 41 us (level)
  no operation moved by 1% of the time
where the time goes in v7:
time: 41 us; the launch traced here: 40.9 us
  Pallas kernels  40.1 us (98%)
  local copies, waits for them, and re-layouts  0.77 us (2%)
    pallas_call x1, Pallas kernels, fused_body(): pl.pallas_call(functools.partial(fused_kernel, nz, nt), out_shape=jax.Sha...  40.1 us

profile of v7, /device:TPU:25, one launch (start us, length us, event | category | flops | bytes accessed | tf_op | source)
XLA Modules:
  0.0 40.9 jit_solution(5949852614539829974)
XLA Ops:
  0.0 40.1 %shard_map.55 = bf16[256,896]{1,0:T(8,128)(2,1)S(1)} custom-call(s32[4]{0:T(128)} %lens_hbm.1, bf16[256,3584]{1,0:T(8,128)(2,1)} %hid_hbm.1, bf16[448,128]{1,0:T(8,128)(2,1)} %wq_hbm.1, bf16[448,256]{1,0:T(8,128)(2,1)} %wkv_hbm.1, bf16[448,128]{1,0:T(8,128)(2,1)} %bitcast.1), custom_call_target="tpu_custom_call" | custom-call | tf_op jit(solution)/shard_map/pallas_call | solution.py:693
  40.1 0.8 %copy.7 = bf16[256,896]{1,0:T(8,128)(2,1)} copy(bf16[256,896]{1,0:T(8,128)(2,1)S(1)} %shard_map.55) | data formatting | bytes 917504
